TPU v7x, 16 devices: a whole 2x2x2 slice. The times are simulated.
16 devices in a mesh: dp: 4 (over z, y), kv: 4 (over x, core).
Axes of the slice: x: 2, y: 2, z: 2, core: 2. Of those that a mesh axis runs over, the one named last changes fastest.
Arguments:
- x_in: bfloat16 [1024, 640], P('dp'), parts along dimension 0
- positions: int32 [1024], P('dp'), parts along dimension 0
- k_cache: bfloat16 [1024, 512, 256], P('dp', 'kv'), parts along dimension 0
- v_cache: bfloat16 [1024, 512, 256], P('dp', 'kv'), parts along dimension 0
- slot_pos: int32 [1024, 512], P('dp', 'kv'), parts along dimension 0
- norm_scale: bfloat16 [640], replicated
- w_q: bfloat16 [640, 1024], replicated
- w_k: bfloat16 [640, 256], replicated
- w_v: bfloat16 [640, 256], replicated
- w_o: bfloat16 [1024, 640], replicated
- b_o: bfloat16 [640], replicated
Outputs:
- output 1: bfloat16 [1024, 640], P('dp'), parts along dimension 0
- output 2: bfloat16 [1024, 512, 256], P('dp', 'kv'), parts along dimension 0
- output 3: bfloat16 [1024, 512, 256], P('dp', 'kv'), parts along dimension 0
- output 4: int32 [1024, 512], P('dp', 'kv'), parts along dimension 0
There are 4 independent parts. A program takes and returns all parts, laid end to end along the dimension named above; an argument that names none is the same for every part.
All inputs are finite; a program needn't handle non-finite values.
Results may differ from a plain program's by a relative error of at most 0.00593895.
Values sent between devices are 32-bit elements.
A program may use at most 1 GiB of HBM per device.

v0:
```python
import jax
import jax.numpy as jnp
from jax import lax
from jax.sharding import PartitionSpec as P

HEAD_DIM = 256
ROPE_DIM = 128
ROPE_BASE = 10000.0
EPS = 1e-6
NEG_LARGE = -1e30
SCORE_SCALE = HEAD_DIM ** -0.5


def rms_norm(x_in, norm_scale):
    x_f32 = x_in.astype(jnp.float32)
    mean_sq = jnp.mean(x_f32 * x_f32, axis=-1, keepdims=True)
    return (x_f32 * lax.rsqrt(mean_sq + EPS) * (1.0 + norm_scale.astype(jnp.float32))).astype(jnp.bfloat16)


def rope_tables(positions):
    rope_half = ROPE_DIM // 2
    inv_freq = ROPE_BASE ** (-jnp.arange(rope_half, dtype=jnp.float32) / rope_half)
    angles = positions.astype(jnp.float32)[:, None] * inv_freq[None, :]
    return jnp.cos(angles), jnp.sin(angles)


def rotate(tensor, cos_t, sin_t):
    rope_half = ROPE_DIM // 2
    rot_first = tensor[..., :rope_half]
    rot_second = tensor[..., rope_half:ROPE_DIM]
    return jnp.concatenate([rot_first * cos_t - rot_second * sin_t, rot_second * cos_t + rot_first * sin_t, tensor[..., ROPE_DIM:]], axis=-1)


def project_query(normed, cos_t, sin_t, w_q):
    q_full = jnp.dot(normed, w_q, preferred_element_type=jnp.float32)
    q_full = q_full.reshape(normed.shape[0], w_q.shape[1] // HEAD_DIM, HEAD_DIM)
    return rotate(q_full, cos_t[:, None, :], sin_t[:, None, :]).astype(jnp.bfloat16)


def project_kv(normed, cos_t, sin_t, w_k, w_v):
    k_new = rotate(jnp.dot(normed, w_k, preferred_element_type=jnp.float32), cos_t, sin_t).astype(jnp.bfloat16)
    v_new = jnp.dot(normed, w_v, preferred_element_type=jnp.float32).astype(jnp.bfloat16)
    return k_new, v_new


def write_slots(k_cache, v_cache, slot_pos, k_new, v_new, positions, slot_offset, window):
    slot_ids = slot_offset + jnp.arange(k_cache.shape[1], dtype=jnp.int32)
    hit_mask = slot_ids[None, :] == jnp.mod(positions, window)[:, None]
    k_out = jnp.where(hit_mask[:, :, None], k_new[:, None, :], k_cache)
    v_out = jnp.where(hit_mask[:, :, None], v_new[:, None, :], v_cache)
    slot_pos_out = jnp.where(hit_mask, positions[:, None], slot_pos)
    return k_out, v_out, slot_pos_out


def usable_slots(slot_pos_out, positions, window):
    slot_age = positions[:, None] - slot_pos_out
    return (slot_pos_out >= 0) & (slot_age >= 0) & (slot_age < window)


def partial_attention(q_rot, k_out, v_out, usable):
    scores = jnp.einsum('bhd,bsd->bhs', q_rot, k_out, preferred_element_type=jnp.float32) * SCORE_SCALE
    scores = jnp.where(usable[:, None, :], scores, NEG_LARGE)
    local_max = jnp.max(scores, axis=-1)
    weights = jnp.where(usable[:, None, :], jnp.exp(scores - local_max[..., None]), 0.0)
    local_sum = jnp.sum(weights, axis=-1)
    local_acc = jnp.einsum('bhs,bsd->bhd', weights.astype(jnp.bfloat16), v_out, preferred_element_type=jnp.float32)
    return local_max, local_sum, local_acc


def residual_out(x_in, attn_rows, w_o, b_o):
    return (x_in.astype(jnp.float32) + jnp.dot(attn_rows, w_o, preferred_element_type=jnp.float32) + b_o.astype(jnp.float32)).astype(jnp.bfloat16)


def solution(mesh):
    kv_size = mesh.shape['kv']
    row_spec = P('dp', None)
    cache_spec = P('dp', 'kv', None)
    slot_spec = P('dp', 'kv')
    vec_spec = P(None)
    mat_spec = P(None, None)

    def local_step(x_in, positions, k_cache, v_cache, slot_pos, norm_scale, w_q, w_k, w_v, w_o, b_o):
        local_slots = k_cache.shape[1]
        window = local_slots * kv_size
        slot_offset = lax.axis_index('kv') * local_slots
        normed = rms_norm(x_in, norm_scale)
        cos_t, sin_t = rope_tables(positions)
        q_rot = project_query(normed, cos_t, sin_t, w_q)
        k_new, v_new = project_kv(normed, cos_t, sin_t, w_k, w_v)
        k_out, v_out, slot_pos_out = write_slots(k_cache, v_cache, slot_pos, k_new, v_new, positions, slot_offset, window)
        usable = usable_slots(slot_pos_out, positions, window)
        local_max, local_sum, local_acc = partial_attention(q_rot, k_out, v_out, usable)
        global_max = lax.pmax(local_max, 'kv')
        factor = jnp.exp(local_max - global_max)
        total_sum, total_acc = lax.psum((local_sum * factor, local_acc * factor[..., None]), 'kv')
        attn_rows = (total_acc / total_sum[..., None]).astype(jnp.bfloat16).reshape(x_in.shape[0], w_q.shape[1])
        x_out = residual_out(x_in, attn_rows, w_o, b_o)
        return x_out, k_out, v_out, slot_pos_out

    return jax.shard_map(
        local_step,
        mesh=mesh,
        in_specs=(row_spec, P('dp'), cache_spec, cache_spec, slot_spec, vec_spec, mat_spec, mat_spec, mat_spec, mat_spec, vec_spec),
        out_specs=(row_spec, cache_spec, cache_spec, slot_spec),
        check_vma=False)
```

profile of v0, /device:TPU:0, one launch (start us, length us, event | category | flops | bytes accessed | tf_op | source)
XLA Modules:
  0.0 121.4 jit_solution(14502461988237859554)
XLA Ops:
  7.2 0.0 copy-start
  7.2 0.0 all-reduce.2.cloned.1.call-start
  7.3 1.2 fusion.3
  8.5 0.8 fusion.26
  9.2 0.7 convert_add_fusion
  9.9 1.4 %convolution_convert_fusion = bf16[256,256]{1,0:T(8,128)(2,1)S(1)} fusion(bf16[640,256]{1,0:T(8,128)(2,1)} %param.19, bf16[256,640]{1,0:T(8,128)(2,1)} %param.11, f32[640]{0:T(1024)S(1)} %convert_add_fusion, f32[256]{0:T(256)S(1)} %add_rsqrt_fusion), kind=kOutput, calls=%fused_computation.8 | convolution fusion | flops 84606976 | bytes 790016 | tf_op jit(solution)/shard_map/dot_general | solution.py:42
  11.3 1.5 %fusion.21 = f32[256,256]{0,1:T(8,128)S(1)} fusion(bf16[640,256]{1,0:T(8,128)(2,1)} %param.18, bf16[256,640]{1,0:T(8,128)(2,1)} %param.11, f32[640]{0:T(1024)S(1)} %convert_add_fusion, f32[256]{0:T(256)S(1)} %add_rsqrt_fusion), kind=kOutput, calls=%fused_computation.49 | convolution fusion | flops 84541440 | bytes 921088 | tf_op jit(solution)/shard_map/dot_general | solution.py:41
  12.8 0.3 multiply_cosine_fusion
  13.1 0.1 copy.15
  13.2 0.1 copy.17
  13.4 0.1 copy.16
  13.5 0.0 copy-done
  13.5 1.6 %fusion.23 = f32[256,1024]{1,0:T(8,128)S(1)} fusion(bf16[640,1024]{1,0:T(8,128)(2,1)S(1)} %copy-done, bf16[256,640]{1,0:T(8,128)(2,1)} %param.11, f32[640]{0:T(1024)S(1)} %convert_add_fusion, f32[256]{0:T(256)S(1)} %add_rsqrt_fusion), kind=kOutput, calls=%fused_computation.50 | convolution fusion | flops 336199680 | bytes 2690560 | tf_op jit(solution)/shard_map/dot_general | solution.py:35
  15.1 0.5 reshape.134
  15.6 0.1 slice.42
  15.7 0.5 subtract_convert_fusion
  16.2 1.7 %compare_and_fusion = (pred[256,128]{1,0:T(8,128)(4,1)S(1)}, s32[256,128]{1,0:T(8,128)}, pred[256,128]{1,0:T(8,128)(4,1)S(1)}) fusion(s32[256]{0:T(256)} %param.12, s32[256,128]{1,0:T(8,128)} %param.15, s32[256]{0:T(256)S(1)} %get-tuple-element.20, s32[128]{0:T(128)S(1)} %iota_add_fusion), kind=kLoop, calls=%fused_computation.32 | loop fusion | flops 262144 | bytes 330240 | tf_op jit(solution)/shard_map/and | solution.py:57
  17.9 23.0 %broadcast_select_fusion.1 = (bf16[256,128,256]{2,1,0:T(8,128)(2,1)}, bf16[256,128,256]{2,1,0:T(8,128)(2,1)}) fusion(bf16[256,128,256]{2,1,0:T(8,128)(2,1)} %param.13, pred[256,128]{1,0:T(8,128)(4,1)S(1)} %get-tuple-element.14, bf16[256,256]{1,0:T(8,128)(2,1)S(1)} %copy.17, bf16[256,128,256]{2,1,0:T(8,128)(2,1)} %param.14, ...), kind=kLoop, calls=%fused_computation.1 | loop fusion | flops 16777216 | bytes 67403776 | tf_op jit(solution)/shard_map/jit(_where)/select_n | solution.py:49
  40.9 10.4 %fusion.27 = (f32[256,4]{1,0:T(8,128)S(1)}, f32[256,4,128]{2,1,0:T(4,128)S(1)}) fusion(bf16[256,128,256]{2,1,0:T(8,128)(2,1)} %get-tuple-element.12, bf16[256,4,128]{2,1,0:T(4,128)(2,1)S(1)} %slice.42, bf16[256,4,64]{2,1,0:T(4,128)(2,1)S(1)} %get-tuple-element.9, bf16[256,4,64]{2,1,0:T(4,128)(2,1)S(1)} %get-tuple-element.8, ...), kind=kOutput, calls=%fused_computation.53 | convolution fusion | flops 69073920 | bytes 17862656 | tf_op jit(solution)/shard_map/bhd,bsd->bhs/dot_general | solution.py:61
  51.3 14.7 %pmax.7 = f32[256,4]{1,0:T(8,128)S(1)} all-reduce(f32[256,4]{1,0:T(8,128)S(1)} %get-tuple-element.21), channel_id=1, replica_groups=mesh['dp'=4,'kv'=4] {'kv'}, use_global_device_ids=true, to_apply=%region_2.3 | all-reduce | flops 1024 | bytes 8192 | tf_op jit(solution)/shard_map/pmax | solution.py:93
  66.0 0.7 fusion.11
  66.8 0.0 copy-start.3
  66.8 0.0 copy-start.1
  66.9 0.0 copy-start.2
  66.9 9.3 %convolution_multiply_fusion = f32[256,4,256]{2,1,0:T(4,128)} fusion(bf16[256,128,256]{2,1,0:T(8,128)(2,1)} %get-tuple-element.13, f32[256,4]{1,0:T(8,128)S(1)} %get-tuple-element.5, f32[256,4,128]{2,1,0:T(4,128)S(1)} %get-tuple-element.22, f32[256,4]{1,0:T(8,128)S(1)} %get-tuple-element.21, pred[256,128]{1,0:T(8,128)(4,1)S(1)} %get-tuple-element.6), kind=kOutput, calls=%fused_computation.2 | convolution fusion | flops 67764224 | bytes 18391040 | tf_op jit(solution)/shard_map/bhs,bsd->bhd/dot_general | solution.py:66
  76.2 0.0 all-reduce.2.cloned.1.call-update
  76.2 0.0 copy-done.3
  76.3 13.6 %psum.15 = f32[256,4]{1,0:T(8,128)S(1)} all-reduce(f32[256,4]{1,0:T(8,128)S(1)} %get-tuple-element.4), channel_id=1, replica_groups=mesh['dp'=4,'kv'=4] {'kv'}, use_global_device_ids=true, to_apply=%region_5.6 | all-reduce | flops 1024 | bytes 8192 | tf_op jit(solution)/shard_map/psum | solution.py:95
  89.9 20.3 %all-reduce.2.cloned.1.call-done = f32[256,4,256]{2,1,0:T(4,128)} async-done(((f32[256,4,256]{2,1,0:T(4,128)}), f32[256,4,256]{2,1,0:T(4,128)}) %all-reduce.2.cloned.1.call-update) | async-done | bytes 1048592 | tf_op jit(solution)/shard_map/psum | solution.py:95
  110.2 1.6 %divide_convert_fusion = bf16[256,4,256]{2,1,0:T(4,128)(2,1)S(1)} fusion(f32[256,4,256]{2,1,0:T(4,128)} %all-reduce.2.cloned.1.call-done, f32[256,4]{1,0:T(8,128)S(1)} %psum.15), kind=kLoop, calls=%fused_computation.9 | loop fusion | flops 524288 | bytes 1576960 | tf_op jit(solution)/shard_map/convert_element_type | solution.py:96
  111.8 0.1 copy.18
  111.9 2.6 %fusion.2 = bf16[256,640]{1,0:T(8,128)(2,1)} fusion(bf16[256,1024]{1,0:T(8,128)(2,1)S(1)} %bitcast.10, bf16[1024,640]{1,0:T(8,128)(2,1)} %param.20, bf16[256,640]{1,0:T(8,128)(2,1)S(1)} %copy-done.2, f32[640]{0:T(1024)S(1)} %convert_element_type.41), kind=kOutput, calls=%fused_computation.7 | convolution fusion | flops 336199680 | bytes 2492928 | tf_op jit(solution)/shard_map/dot_general | solution.py:71
  (9 shorter events, 0.1 us)
Async XLA Ops:
  7.2 6.3 %copy-start = (bf16[640,1024]{1,0:T(8,128)(2,1)S(1)}, bf16[640,1024]{1,0:T(8,128)(2,1)}, u32[]{:S(2)}) copy-start(bf16[640,1024]{1,0:T(8,128)(2,1)} %param.17) | copy-start | bytes 3932164
  7.2 103.0 %all-reduce.2.cloned.1.call-start = ((), (), s32[]{:S(2)}) async-start(), calls=%async_computation | async-start | bytes 2097152 | tf_op jit(solution)/shard_map/psum | solution.py:95
  66.8 9.4 %copy-start.3 = (bf16[640]{0:T(1024)(128)(2,1)S(1)}, bf16[640]{0:T(1024)(128)(2,1)}, u32[]{:S(2)}) copy-start(bf16[640]{0:T(1024)(128)(2,1)} %param.21) | copy-start | bytes 3844
  66.8 47.7 %copy-start.1 = (bf16[640,1024]{1,0:T(8,128)(2,1)S(1)}, bf16[640,1024]{1,0:T(8,128)(2,1)}, u32[]{:S(2)}) copy-start(bf16[640,1024]{1,0:T(8,128)(2,1)} %param.17) | copy-start | bytes 3932164
  66.9 45.0 %copy-start.2 = (bf16[256,640]{1,0:T(8,128)(2,1)S(1)}, bf16[256,640]{1,0:T(8,128)(2,1)}, u32[]{:S(2)}) copy-start(bf16[256,640]{1,0:T(8,128)(2,1)} %param.11) | copy-start | bytes 983044
Sparse Core Ops, SparseCore 0:
  76.4 33.8 all-reduce.1
where the time goes:
time: 122 us; the launch traced here: 121 us
  other arithmetic  30.6 us (25%)
  blocking collectives  28.3 us (23%)
  matrix products  26.8 us (22%)
  waiting for transfers between devices  20.4 us (17%)
  between operations  14.3 us (12%)
    select_n x1, other arithmetic, write_slots(): k_out = jnp.where(hit_mask[:, :, None], k_new[:, None, :], k_cache)  23 us
    psum x1, waiting for transfers between devices, local_step(): lax.psum((local_sum * factor, local_acc * factor[..., None]), 'kv')  20.3 us
    pmax x1, blocking collectives, local_step(): global_max = lax.pmax(local_max, 'kv')  14.7 us
    psum x1, blocking collectives, local_step(): lax.psum((local_sum * factor, local_acc * factor[..., None]), 'kv')  13.6 us
    dot_general x1, matrix products, partial_attention(): jnp.einsum('bhd,bsd->bhs', q_rot, k_out, preferred_element_type=jnp.float32)  10.4 us
    dot_general x1, matrix products, partial_attention(): jnp.einsum('bhs,bsd->bhd', weights.astype(jnp.bfloat16), v_out, preferred...  9.34 us
    dot_general x1, matrix products, residual_out(): jnp.dot(attn_rows, w_o, preferred_element_type=jnp.float32)  2.62 us
  transfers between devices with their start and end apart: 1, of which 1 were waited for; matrix products, arithmetic and copies ran while one was open for 0% of the time, Pallas kernels for 0%

commit v1 on v0

v1 whole, which is shorter than its diff:
```python
import functools
import numpy as np
import jax
import jax.numpy as jnp
from jax import lax
from jax.experimental import pallas as pl
from jax.experimental.pallas import tpu as pltpu
from jax.sharding import PartitionSpec as P

HEADS = 4
HEAD_DIM = 256
ROPE_DIM = 128
ROPE_BASE = 10000.0
EPS = 1e-6
NEG_LARGE = -1e30
SCORE_SCALE = HEAD_DIM ** -0.5

UNIT = 8
CHUNK_UNITS = 4
ROWS = UNIT * HEADS
PACKET = 2 * ROWS + 8
PIECES = 2
AHEAD = 3
MESH = pl.DeviceIdType.MESH
F32 = jnp.float32
BF16 = jnp.bfloat16


def attend_kernel(window, pos_h, freq_h, x_h, ns_h, wk_h, wv_h, wq_h, sp_h, wo_h, bo_h, k_h, v_h,
                  *rest):
    k_vm, v_vm = rest[:PIECES], rest[PIECES:2 * PIECES]
    (x_new, k_new, v_new, sp_new,
                  pos, freq, x_in, ns, wk, wv, wq, sp, wo, bo,
                  pos_b, x_f, q_s, pk, rc1, cm, rc2, o_s, ag,
                  in_sem, k_sem, v_sem, s1, r1, s2, r2, sa, ra, sb, rb, sc, rc) = rest[2 * PIECES:]
    me = lax.axis_index('kv')
    x_side, core = me // 2, me % 2
    over = {'kv': 2 * (1 - x_side) + core}
    beside = {'kv': 2 * x_side + 1 - core}
    over_i = 2 * (1 - x_side) + core
    batch, slots = sp.shape
    chunk = UNIT * CHUNK_UNITS
    chunks = batch // chunk
    half = chunks // 2

    barrier = pltpu.get_barrier_semaphore()
    pl.semaphore_signal(barrier, inc=1, device_id=over, device_id_type=MESH)
    pl.semaphore_signal(barrier, inc=1, device_id=beside, device_id_type=MESH)

    smalls = [pltpu.make_async_copy(src, dst, in_sem.at[n]) for n, (src, dst) in enumerate((
        (pos_h, pos), (freq_h, freq), (x_h, x_in), (ns_h, ns), (wk_h, wk), (wv_h, wv), (wq_h, wq), (sp_h, sp), (wo_h, wo), (bo_h, bo)))]

    span = chunks // PIECES

    def cache_copy(j, piece):
        rows, held = pl.ds(j * chunk, chunk), pl.ds((j - piece * span) * chunk, chunk)
        return (pltpu.make_async_copy(k_h.at[rows], k_vm[piece].at[held], k_sem.at[j]),
                pltpu.make_async_copy(v_h.at[rows], v_vm[piece].at[held], v_sem.at[j]))

    for small in smalls[:8]:
        small.start()
    for j in range(AHEAD):
        for copy in cache_copy(j, j // span):
            copy.start()
    for small in smalls[8:]:
        small.start()

    smalls[0].wait()
    smalls[1].wait()
    for r in range(batch // 128):
        row = pos[r:r + 1, :].astype(F32)
        pos_b[pl.ds(128 * r, 128), :] = jnp.transpose(jnp.broadcast_to(row, (128, 128)))
    angles = pos_b[...] * freq[...]
    low = lax.broadcasted_iota(jnp.int32, (batch, 128), 1) < ROPE_DIM // 2
    cos_t = jnp.cos(angles)
    sin_t = jnp.sin(angles)
    sin_t = jnp.where(low, -sin_t, sin_t)

    def rotate(first):
        return first * cos_t + pltpu.roll(first, ROPE_DIM // 2, 1) * sin_t

    smalls[2].wait()
    smalls[3].wait()
    x32 = x_in[...].astype(F32)
    x_f[...] = x32
    mean_sq = jnp.mean(x32 * x32, axis=-1, keepdims=True)
    normed = (x32 * lax.rsqrt(mean_sq + EPS) * (1.0 + ns[...].astype(F32))).astype(BF16)
    smalls[4].wait()
    smalls[5].wait()
    k_row = jnp.dot(normed, wk[...], preferred_element_type=F32)
    k_new[:, :128] = rotate(k_row[:, :128]).astype(BF16).astype(F32)
    k_new[:, 128:] = k_row[:, 128:].astype(BF16).astype(F32)
    v_new[...] = jnp.dot(normed, wv[...], preferred_element_type=F32).astype(BF16).astype(F32)
    smalls[6].wait()
    for h in range(HEADS):
        q_row = jnp.dot(normed, wq[:, h * HEAD_DIM:(h + 1) * HEAD_DIM], preferred_element_type=F32)
        q_s[:, h, :, :128] = rotate(q_row[:, :128]).reshape(batch // UNIT, UNIT, 128)
        q_s[:, h, :, 128:] = q_row[:, 128:].reshape(batch // UNIT, UNIT, 128)
    smalls[7].wait()
    pl.semaphore_wait(barrier, 2)

    lane = lax.broadcasted_iota(jnp.int32, (UNIT, 128), 1)
    row_seq = lax.broadcasted_iota(jnp.int32, (ROWS, 128), 0) % UNIT

    def scores_of(u, piece):
        keys = k_vm[piece][pl.ds(u * UNIT - piece * span * chunk, UNIT)].reshape(UNIT * slots, HEAD_DIM)
        q_b = q_s[u].reshape(ROWS, HEAD_DIM).astype(BF16)
        return q_b, lax.dot_general(q_b, keys, (((1,), (1,)), ((), ())), preferred_element_type=F32)

    def weights_of(u, q_b, all_scores):
        seqs = pl.ds(u * UNIT, UNIT)
        scores = all_scores[:, :slots]
        for s in range(1, UNIT):
            scores = jnp.where(row_seq == s, all_scores[:, s * slots:(s + 1) * slots], scores)
        p_now = pos_b[seqs, :].astype(jnp.int32)
        slot = (p_now & (window - 1)) - me * slots
        hit = lane == slot
        held = jnp.where(hit, p_now, sp[seqs, :])
        sp_new[seqs, :] = held
        age = p_now - held
        usable = (held >= 0) & (age >= 0) & (age < window)
        fresh = jnp.sum(q_b.astype(F32).reshape(HEADS, UNIT, HEAD_DIM) * k_new[seqs, :][None], axis=-1, keepdims=True)
        scores = jnp.where(hit[None], fresh, scores.reshape(HEADS, UNIT, slots)) * SCORE_SCALE
        scores = jnp.where(usable[None], scores, NEG_LARGE)
        top = jnp.max(scores, axis=-1, keepdims=True)
        weights = jnp.where(usable[None], jnp.exp(scores - top), 0.0)
        total = jnp.sum(weights, axis=-1, keepdims=True)
        fresh_weight = jnp.sum(jnp.where(hit[None], weights, 0.0), axis=-1, keepdims=True)
        kept = jnp.where(hit[None], 0.0, weights).reshape(ROWS, slots)
        spread = jnp.concatenate([jnp.where(row_seq == s, kept, 0.0).astype(BF16) for s in range(UNIT)], axis=1)
        return top, total, fresh_weight, spread

    def sums_of(u, piece, fresh_weight, spread):
        values = v_vm[piece][pl.ds(u * UNIT - piece * span * chunk, UNIT)].reshape(UNIT * slots, HEAD_DIM)
        sums = jnp.dot(spread, values, preferred_element_type=F32).reshape(HEADS, UNIT, HEAD_DIM)
        sums = sums + fresh_weight.astype(BF16).astype(F32) * v_new[pl.ds(u * UNIT, UNIT), :][None]
        return sums.reshape(ROWS, HEAD_DIM)

    def attend(j, piece):
        units = [j * CHUNK_UNITS + i for i in range(CHUNK_UNITS)]
        scored = [scores_of(u, piece) for u in units]
        weighed = [weights_of(u, *pair) for u, pair in zip(units, scored)]
        for i, u in enumerate(units):
            top, total, fresh_weight, spread = weighed[i]
            sums = sums_of(u, piece, fresh_weight, spread)
            pk[j, i, 0:ROWS, :] = sums[:, :128]
            pk[j, i, ROWS:2 * ROWS, :] = sums[:, 128:]
            tile = jnp.zeros((UNIT, 128), F32)
            for h in range(HEADS):
                tile = jnp.where(lane == h, top[h], jnp.where(lane == HEADS + h, total[h], tile))
            pk[j, i, 2 * ROWS:, :] = tile

    def merge(a, b):
        ta, tb = a[2 * ROWS:, :], b[2 * ROWS:, :]
        tile = jnp.maximum(ta, tb)
        ea, eb = jnp.exp(ta - tile), jnp.exp(tb - tile)
        parts, totals = [], []
        for h in range(HEADS):
            fa, fb = ea[:, h:h + 1], eb[:, h:h + 1]
            totals.append(fa * ta[:, HEADS + h:HEADS + h + 1] + fb * tb[:, HEADS + h:HEADS + h + 1])
            parts.append([fa * a[o + h * UNIT:o + (h + 1) * UNIT, :] + fb * b[o + h * UNIT:o + (h + 1) * UNIT, :] for o in (0, ROWS)])
        return tile, parts, totals

    def first_copy(j):
        return pltpu.make_async_remote_copy(pk.at[j, pl.ds(2 * (1 - core), 2)], rc1.at[j], s1.at[j], r1.at[j], device_id=beside, device_id_type=MESH)

    def second_copy(j):
        return pltpu.make_async_remote_copy(cm.at[j, 1 - x_side], rc2.at[j], s2.at[j], r2.at[j], device_id=over, device_id_type=MESH)

    def first_merge(j):
        first_copy(j).wait_recv()
        for i in range(2):
            tile, parts, totals = merge(pk[j, 2 * core + i], rc1[j, i])
            for h in range(HEADS):
                cm[j, i, h * UNIT:(h + 1) * UNIT, :] = parts[h][0]
                cm[j, i, ROWS + h * UNIT:ROWS + (h + 1) * UNIT, :] = parts[h][1]
                tile = jnp.where(lane == HEADS + h, totals[h], tile)
            cm[j, i, 2 * ROWS:, :] = tile
        second_copy(j).start()

    def second_merge(j):
        second_copy(j).wait_recv()
        _, parts, totals = merge(cm[j, x_side], rc2[j])
        rows = pl.ds(j * UNIT, UNIT)
        for h in range(HEADS):
            inverse = 1.0 / totals[h]
            o_s[rows, h * HEAD_DIM:h * HEAD_DIM + 128] = parts[h][0] * inverse
            o_s[rows, h * HEAD_DIM + 128:(h + 1) * HEAD_DIM] = parts[h][1] * inverse

    own_unit = 2 * core + x_side

    def gather_copy(g, owner, target, send, recv):
        rows = ag.at[owner, pl.ds(g * half * UNIT, half * UNIT)]
        return pltpu.make_async_remote_copy(rows, rows, send.at[g], recv.at[g], device_id=target, device_id_type=MESH)

    def project(g):
        o_b = o_s[pl.ds(g * half * UNIT, half * UNIT), :].astype(BF16)
        rows = jnp.concatenate([x_f[pl.ds((g * half + i) * chunk + own_unit * UNIT, UNIT), :] for i in range(half)], axis=0)
        ag[me, pl.ds(g * half * UNIT, half * UNIT), :] = rows + jnp.dot(o_b, wo[...], preferred_element_type=F32) + bo[...].astype(F32)
        gather_copy(g, me, over, sa, ra).start()
        gather_copy(g, me, beside, sb, rb).start()

    def forward(g):
        gather_copy(g, me, over, sa, ra).wait_recv()
        gather_copy(g, over_i, beside, sc, rc).start()

    def step(piece, j, carry):
        for ahead in range(PIECES):
            @pl.when((j + AHEAD < chunks) & ((j + AHEAD) // span == ahead))
            def _():
                for copy in cache_copy(j + AHEAD, ahead):
                    copy.start()
        for copy in cache_copy(j, piece):
            copy.wait()
        attend(j, piece)
        first_copy(j).start()

        @pl.when(j >= 1)
        def _():
            first_merge(j - 1)

        @pl.when(j >= 3)
        def _():
            second_merge(j - 3)

        @pl.when(j == half + 2)
        def _():
            smalls[8].wait()
            smalls[9].wait()
            project(0)

        return carry

    for piece in range(PIECES):
        lax.fori_loop(piece * span, (piece + 1) * span, functools.partial(step, piece), 0)
    second_merge(chunks - 3)
    forward(0)
    first_merge(chunks - 1)
    second_merge(chunks - 2)
    second_merge(chunks - 1)
    project(1)
    forward(1)
    for g in range(2):
        gather_copy(g, me, beside, sb, rb).wait_recv()
        gather_copy(g, me, beside, sc, rc).wait_recv()
    for c in range(2):
        for j in range(chunks):
            rows = [ag[2 * s + c, j * UNIT:(j + 1) * UNIT, :] for s in range(2)]
            x_new[j * chunk + 2 * UNIT * c:j * chunk + 2 * UNIT * (c + 1), :] = jnp.concatenate(rows, axis=0).astype(BF16)

    def drain(j, carry):
        first_copy(j).wait_send()
        second_copy(j).wait_send()
        return carry

    lax.fori_loop(0, chunks, drain, 0)
    for g in range(2):
        gather_copy(g, me, over, sa, ra).wait_send()
        gather_copy(g, me, beside, sb, rb).wait_send()
        gather_copy(g, over_i, beside, sc, rc).wait_send()


def write_kernel(window, pos, k_new, v_new, x_new, sp_new, *rest):
    k_vm, v_vm = rest[:PIECES], rest[PIECES:2 * PIECES]
    x_out, k_out, v_out, sp_out, k_ring, v_ring, sems, k_sem, v_sem = rest[2 * PIECES:]
    me = lax.axis_index('kv')
    part, slots, _ = k_vm[0].shape
    batch = part * PIECES
    depth, chunk = k_ring.shape[:2]
    chunks = batch // chunk
    span = chunks // PIECES
    others = (pltpu.make_async_copy(x_new, x_out, sems.at[0]), pltpu.make_async_copy(sp_new, sp_out, sems.at[1]))
    for copy in others:
        copy.start()
    tile_row = lax.broadcasted_iota(jnp.int32, (16, HEAD_DIM), 0)

    def copies(j):
        rows, ring = pl.ds(j * chunk, chunk), lax.rem(j, depth)
        return (pltpu.make_async_copy(k_ring.at[ring], k_out.at[rows], k_sem.at[ring]),
                pltpu.make_async_copy(v_ring.at[ring], v_out.at[rows], v_sem.at[ring]))

    def step(piece, j, carry):
        ring = lax.rem(j, depth)

        @pl.when(j >= depth)
        def _():
            for copy in copies(j - depth):
                copy.wait()

        def group(i, carry):
            for n in range(8):
                row = i * 8 + n
                b = j * chunk + row
                slot = (pos[b] & (window - 1)) - me * slots
                base = pl.multiple_of((jnp.clip(slot, 0, slots - 1) // 16) * 16, 16)
                for new, cache, out in ((k_new, k_vm[piece], k_ring), (v_new, v_vm[piece], v_ring)):
                    out[ring, row] = cache[b - piece * part]
                    fresh = jnp.broadcast_to(new[pl.ds(b, 1), :], (16, HEAD_DIM))
                    old = cache[b - piece * part, pl.ds(base, 16), :].astype(F32)
                    out[ring, row, pl.ds(base, 16), :] = jnp.where(tile_row == slot - base, fresh, old).astype(BF16)
            return carry
        lax.fori_loop(0, chunk // 8, group, 0)
        for copy in copies(j):
            copy.start()
        return carry

    for piece in range(PIECES):
        lax.fori_loop(piece * span, (piece + 1) * span, functools.partial(step, piece), 0)
    for j in range(chunks - depth, chunks):
        for copy in copies(j):
            copy.wait()
    for copy in others:
        copy.wait()


def solution(mesh):
    kv_size = mesh.shape['kv']
    row_spec = P('dp', None)
    cache_spec = P('dp', 'kv', None)
    slot_spec = P('dp', 'kv')
    vec_spec = P(None)
    mat_spec = P(None, None)
    half_dims = ROPE_DIM // 2
    freq_row = np.tile(ROPE_BASE ** (-np.arange(half_dims) / half_dims), 2).astype(np.float32)[None, :]

    def local_step(x_in, positions, k_cache, v_cache, slot_pos, norm_scale, w_q, w_k, w_v, w_o, b_o):
        batch, model = x_in.shape
        slots = k_cache.shape[1]
        window = slots * kv_size
        width = w_q.shape[1]
        chunks = batch // (UNIT * CHUNK_UNITS)
        hbm = pl.BlockSpec(memory_space=pltpu.HBM)
        vmem = pl.BlockSpec(memory_space=pltpu.VMEM)
        smem = pl.BlockSpec(memory_space=pltpu.SMEM)
        dma = pltpu.SemaphoreType.DMA
        per_chunk = [dma((chunks,))] * 4
        *held, x_new, k_new, v_new, sp_new = pl.pallas_call(
            functools.partial(attend_kernel, window),
            out_shape=(*([pltpu.VMEM((batch // PIECES, slots, HEAD_DIM), BF16)] * (2 * PIECES)), pltpu.VMEM((batch, model), BF16),
                       pltpu.VMEM((batch, HEAD_DIM), F32), pltpu.VMEM((batch, HEAD_DIM), F32), pltpu.VMEM((batch, slots), jnp.int32)),
            in_specs=[hbm] * 12,
            out_specs=(vmem,) * (2 * PIECES + 4),
            scratch_shapes=[
                pltpu.VMEM((batch // 128, 128), jnp.int32), pltpu.VMEM((1, 128), F32), pltpu.VMEM((batch, model), BF16), pltpu.VMEM((1, model), BF16),
                pltpu.VMEM((model, HEAD_DIM), BF16), pltpu.VMEM((model, HEAD_DIM), BF16), pltpu.VMEM((model, width), BF16),
                pltpu.VMEM((batch, slots), jnp.int32), pltpu.VMEM((width, model), BF16), pltpu.VMEM((1, model), BF16),
                pltpu.VMEM((batch, 128), F32), pltpu.VMEM((batch, model), F32), pltpu.VMEM((batch // UNIT, HEADS, UNIT, HEAD_DIM), F32),
                pltpu.VMEM((chunks, CHUNK_UNITS, PACKET, 128), F32), pltpu.VMEM((chunks, 2, PACKET, 128), F32),
                pltpu.VMEM((chunks, 2, PACKET, 128), F32), pltpu.VMEM((chunks, PACKET, 128), F32),
                pltpu.VMEM((chunks * UNIT, width), F32), pltpu.VMEM((kv_size, chunks * UNIT, model), F32),
                dma((10,)), dma((chunks,)), dma((chunks,)), *per_chunk, *([dma((2,))] * 6)],
            compiler_params=pltpu.CompilerParams(vmem_limit_bytes=16 << 20, collective_id=0, has_side_effects=True),
            name='attend',
        )(*[pltpu.with_memory_space_constraint(a, pltpu.HBM) for a in (
            positions.reshape(batch // 128, 128), jnp.asarray(freq_row), x_in, norm_scale.reshape(1, model), w_k, w_v, w_q, slot_pos,
            w_o, b_o.reshape(1, model), k_cache, v_cache)])
        x_out, k_out, v_out, slot_pos_out = pl.pallas_call(
            functools.partial(write_kernel, window),
            out_shape=(jax.ShapeDtypeStruct((batch, model), BF16), jax.ShapeDtypeStruct(k_cache.shape, BF16),
                       jax.ShapeDtypeStruct(v_cache.shape, BF16), jax.ShapeDtypeStruct((batch, slots), jnp.int32)),
            in_specs=[smem] + [vmem] * (2 * PIECES + 4),
            out_specs=(hbm,) * 4,
            scratch_shapes=[pltpu.VMEM((4, 16, slots, HEAD_DIM), BF16), pltpu.VMEM((4, 16, slots, HEAD_DIM), BF16), dma((2,)), dma((4,)), dma((4,))],
            compiler_params=pltpu.CompilerParams(vmem_limit_bytes=9 << 20),
            name='write',
        )(positions, k_new, v_new, x_new, sp_new, *held)
        return x_out, k_out, v_out, slot_pos_out

    return jax.shard_map(
        local_step,
        mesh=mesh,
        in_specs=(row_spec, P('dp'), cache_spec, cache_spec, slot_spec, vec_spec, mat_spec, mat_spec, mat_spec, mat_spec, vec_spec),
        out_specs=(row_spec, cache_spec, cache_spec, slot_spec),
        check_vma=False)
```

time: 122 us -> 43.4 us (0.36)
  Pallas kernels: 0 us -> 40 us
  other arithmetic: 30.6 us -> 0 us
  blocking collectives: 28.3 us -> 0 us
  matrix products: 26.8 us -> 0 us
  waiting for transfers between devices: 20.4 us -> 0 us
  between operations: 14.3 us -> 0.65 us
  local copies, waits for them, and re-layouts: 1 us -> 2.53 us
    pallas_call x0 -> x2, Pallas kernels: none -> 40 us  [the longest x1 28.2 us: local_step(): pl.pallas_call(functools.partial(attend_kernel, window), out_shape=(*[plt...]
    dot_general x6 -> x0, matrix products: 26.8 us -> none  [the longest x1 10.4 us: partial_attention(): jnp.einsum('bhd,bsd->bhs', q_rot, k_out, preferred_element_type=jnp.float32)]
    select_n x1 -> x0, other arithmetic: 23 us -> none  [write_slots(): k_out = jnp.where(hit_mask[:, :, None], k_new[:, None, :], k_cache)]
    psum x1 -> x0, waiting for transfers between devices: 20.3 us -> none  [local_step(): lax.psum((local_sum * factor, local_acc * factor[..., None]), 'kv')]
    pmax x1 -> x0, blocking collectives: 14.7 us -> none  [local_step(): global_max = lax.pmax(local_max, 'kv')]
    psum x1 -> x0, blocking collectives: 13.6 us -> none  [local_step(): lax.psum((local_sum * factor, local_acc * factor[..., None]), 'kv')]
    convert_element_type x3 -> x0, other arithmetic: 2.33 us -> none  [the longest x1 1.56 us: local_step(): (total_acc / total_sum[..., None]).astype(jnp.bfloat16)]
    reshape x1 -> x2, local copies, waits for them, and re-layouts: 0.5 us -> 2.52 us  [the longest x1 1.26 us: local_step(): norm_scale.reshape(1, model)]
  transfers between devices with their start and end apart: 1 -> 0, of which waited for: 1 -> 0; matrix products, arithmetic and copies ran while one was open for 0% -> 0% of each run, Pallas kernels for 0% -> 0%
where the time goes in v1:
time: 43.4 us; the launch traced here: 43.2 us
  Pallas kernels  40 us (92%)
  local copies, waits for them, and re-layouts  2.53 us (6%)
  between operations  0.65 us (1%)
    pallas_call x1, Pallas kernels, local_step(): pl.pallas_call(functools.partial(attend_kernel, window), out_shape=(*[plt...  28.2 us
    pallas_call x1, Pallas kernels, local_step(): pl.pallas_call(functools.partial(write_kernel, window), out_shape=(jax.Sh...  11.8 us
    reshape x1, local copies, waits for them, and re-layouts, local_step(): norm_scale.reshape(1, model)  1.26 us
    reshape x1, local copies, waits for them, and re-layouts, local_step(): b_o.reshape(1, model)  1.26 us

profile of v1, /device:TPU:0, one launch (start us, length us, event | category | flops | bytes accessed | tf_op | source)
XLA Modules:
  0.0 43.2 jit_solution(17055749044763008135)
XLA Ops:
  0.6 1.3 %reshape.18.ns_h = bf16[1,640]{1,0:T(2,128)(2,1)} reshape(bf16[640]{0:T(1024)(128)(2,1)} %param.17) | data formatting | bytes 2560 | tf_op jit(solution)/shard_map/reshape | solution.py:355
  1.9 1.3 %reshape.19.bo_h = bf16[1,640]{1,0:T(2,128)(2,1)} reshape(bf16[640]{0:T(1024)(128)(2,1)} %param.22) | data formatting | bytes 2560 | tf_op jit(solution)/shard_map/reshape | solution.py:356
  3.2 0.0 copy-start
  3.2 28.2 %attend.1 = (bf16[128,128,256]{2,1,0:T(8,128)(2,1)S(1)}, bf16[128,128,256]{2,1,0:T(8,128)(2,1)S(1)}, bf16[128,128,256]{2,1,0:T(8,128)(2,1)S(1)}, bf16[128,128,25...) custom-call(s32[2,128]{1,0:T(2,128)} %bitcast.1, ...), custom_call_target="tpu_custom_call" | custom-call | tf_op jit(solution)/shard_map/attend/pallas_call | solution.py:337
  31.4 0.0 copy-done
  31.4 11.8 %write.1 = (bf16[256,640]{1,0:T(8,128)(2,1)}, bf16[256,128,256]{2,1,0:T(8,128)(2,1)}, bf16[256,128,256]{2,1,0:T(8,128)(2,1)}, s32[256,128]{1,0:T(8,128)}) custom-call(s32[256]{0:T(256)S(1)} %copy-done, f32[256,256]{1,0:T(8,128)S(1)} %get-tuple-element.12.k_new, f32[256,256]{1,0:T(8,128)S(1)} %get-tuple-element.13.v_new, ...), custom_call_target="tpu_custom_call" | custom-call | tf_op jit(solution)/shard_map/write/pallas_call | solution.py:357
Async XLA Ops:
  3.2 28.2 %copy-start = (s32[256]{0:T(256)S(1)}, s32[256]{0:T(256)}, u32[]{:S(2)}) copy-start(s32[256]{0:T(256)} %pos.1) | copy-start | bytes 3076

commit v2 on v1

--- a/solution.py
+++ b/solution.py
@@ -57,13 +57,14 @@
         return (pltpu.make_async_copy(k_h.at[rows], k_vm[piece].at[held], k_sem.at[j]),
                 pltpu.make_async_copy(v_h.at[rows], v_vm[piece].at[held], v_sem.at[j]))
 
+    def read_ahead(first, last):
+        for j in range(first, last):
+            for copy in cache_copy(j, j // span):
+                copy.start()
+
     for small in smalls[:8]:
         small.start()
-    for j in range(AHEAD):
-        for copy in cache_copy(j, j // span):
-            copy.start()
-    for small in smalls[8:]:
-        small.start()
+    read_ahead(0, AHEAD)
 
     smalls[0].wait()
     smalls[1].wait()
@@ -79,12 +80,13 @@
     def rotate(first):
         return first * cos_t + pltpu.roll(first, ROPE_DIM // 2, 1) * sin_t
 
+    read_ahead(AHEAD, AHEAD + 1)
     smalls[2].wait()
     smalls[3].wait()
     x32 = x_in[...].astype(F32)
     x_f[...] = x32
     mean_sq = jnp.mean(x32 * x32, axis=-1, keepdims=True)
-    normed = (x32 * lax.rsqrt(mean_sq + EPS) * (1.0 + ns[...].astype(F32))).astype(BF16)
+    normed = (x32 * lax.rsqrt(mean_sq + EPS) * (1.0 + ns[...].astype(F32)[None, :])).astype(BF16)
     smalls[4].wait()
     smalls[5].wait()
     k_row = jnp.dot(normed, wk[...], preferred_element_type=F32)
@@ -92,6 +94,9 @@
     k_new[:, 128:] = k_row[:, 128:].astype(BF16).astype(F32)
     v_new[...] = jnp.dot(normed, wv[...], preferred_element_type=F32).astype(BF16).astype(F32)
     smalls[6].wait()
+    read_ahead(AHEAD + 1, chunks)
+    for small in smalls[8:]:
+        small.start()
     for h in range(HEADS):
         q_row = jnp.dot(normed, wq[:, h * HEAD_DIM:(h + 1) * HEAD_DIM], preferred_element_type=F32)
         q_s[:, h, :, :128] = rotate(q_row[:, :128]).reshape(batch // UNIT, UNIT, 128)
@@ -196,7 +201,7 @@
     def project(g):
         o_b = o_s[pl.ds(g * half * UNIT, half * UNIT), :].astype(BF16)
         rows = jnp.concatenate([x_f[pl.ds((g * half + i) * chunk + own_unit * UNIT, UNIT), :] for i in range(half)], axis=0)
-        ag[me, pl.ds(g * half * UNIT, half * UNIT), :] = rows + jnp.dot(o_b, wo[...], preferred_element_type=F32) + bo[...].astype(F32)
+        ag[me, pl.ds(g * half * UNIT, half * UNIT), :] = rows + jnp.dot(o_b, wo[...], preferred_element_type=F32) + bo[...].astype(F32)[None, :]
         gather_copy(g, me, over, sa, ra).start()
         gather_copy(g, me, beside, sb, rb).start()
 
@@ -205,11 +210,6 @@
         gather_copy(g, over_i, beside, sc, rc).start()
 
     def step(piece, j, carry):
-        for ahead in range(PIECES):
-            @pl.when((j + AHEAD < chunks) & ((j + AHEAD) // span == ahead))
-            def _():
-                for copy in cache_copy(j + AHEAD, ahead):
-                    copy.start()
         for copy in cache_copy(j, piece):
             copy.wait()
         attend(j, piece)
@@ -341,9 +341,9 @@
             in_specs=[hbm] * 12,
             out_specs=(vmem,) * (2 * PIECES + 4),
             scratch_shapes=[
-                pltpu.VMEM((batch // 128, 128), jnp.int32), pltpu.VMEM((1, 128), F32), pltpu.VMEM((batch, model), BF16), pltpu.VMEM((1, model), BF16),
+                pltpu.VMEM((batch // 128, 128), jnp.int32), pltpu.VMEM((1, 128), F32), pltpu.VMEM((batch, model), BF16), pltpu.VMEM((model,), BF16),
                 pltpu.VMEM((model, HEAD_DIM), BF16), pltpu.VMEM((model, HEAD_DIM), BF16), pltpu.VMEM((model, width), BF16),
-                pltpu.VMEM((batch, slots), jnp.int32), pltpu.VMEM((width, model), BF16), pltpu.VMEM((1, model), BF16),
+                pltpu.VMEM((batch, slots), jnp.int32), pltpu.VMEM((width, model), BF16), pltpu.VMEM((model,), BF16),
                 pltpu.VMEM((batch, 128), F32), pltpu.VMEM((batch, model), F32), pltpu.VMEM((batch // UNIT, HEADS, UNIT, HEAD_DIM), F32),
                 pltpu.VMEM((chunks, CHUNK_UNITS, PACKET, 128), F32), pltpu.VMEM((chunks, 2, PACKET, 128), F32),
                 pltpu.VMEM((chunks, 2, PACKET, 128), F32), pltpu.VMEM((chunks, PACKET, 128), F32),
@@ -352,8 +352,8 @@
             compiler_params=pltpu.CompilerParams(vmem_limit_bytes=16 << 20, collective_id=0, has_side_effects=True),
             name='attend',
         )(*[pltpu.with_memory_space_constraint(a, pltpu.HBM) for a in (
-            positions.reshape(batch // 128, 128), jnp.asarray(freq_row), x_in, norm_scale.reshape(1, model), w_k, w_v, w_q, slot_pos,
-            w_o, b_o.reshape(1, model), k_cache, v_cache)])
+            positions.reshape(batch // 128, 128), jnp.asarray(freq_row), x_in, norm_scale, w_k, w_v, w_q, slot_pos,
+            w_o, b_o, k_cache, v_cache)])
         x_out, k_out, v_out, slot_pos_out = pl.pallas_call(
             functools.partial(write_kernel, window),
             out_shape=(jax.ShapeDtypeStruct((batch, model), BF16), jax.ShapeDtypeStruct(k_cache.shape, BF16),

time: 43.4 us -> 41.6 us (0.959)
  local copies, waits for them, and re-layouts: 2.53 us -> 0.01 us
  Pallas kernels: 40 us -> 40.9 us
    reshape x2 -> x0, local copies, waits for them, and re-layouts: 2.52 us -> none  [the longest x1 1.26 us: local_step(): norm_scale.reshape(1, model)]
    pallas_call x1, Pallas kernels: 28.2 us -> 29.1 us  [local_step(): pl.pallas_call(functools.partial(attend_kernel, window), out_shape=(*[plt...]
where the time goes in v2:
time: 41.6 us; the launch traced here: 41.5 us
  Pallas kernels  40.9 us (98%)
  between operations  0.66 us (2%)
    pallas_call x1, Pallas kernels, local_step(): pl.pallas_call(functools.partial(attend_kernel, window), out_shape=(*[plt...  29.1 us
    pallas_call x1, Pallas kernels, local_step(): pl.pallas_call(functools.partial(write_kernel, window), out_shape=(jax.Sh...  11.8 us

profile of v2, /device:TPU:0, one launch (start us, length us, event | category | flops | bytes accessed | tf_op | source)
XLA Modules:
  0.0 41.5 jit_solution(9684258459828637185)
XLA Ops:
  0.6 0.0 copy-start
  0.6 29.1 %attend.1 = (bf16[128,128,256]{2,1,0:T(8,128)(2,1)S(1)}, bf16[128,128,256]{2,1,0:T(8,128)(2,1)S(1)}, bf16[128,128,256]{2,1,0:T(8,128)(2,1)S(1)}, bf16[128,128,25...) custom-call(s32[2,128]{1,0:T(2,128)} %bitcast.1, ...), custom_call_target="tpu_custom_call" | custom-call | tf_op jit(solution)/shard_map/attend/pallas_call | solution.py:337
  29.7 0.0 copy-done
  29.7 11.8 %write.1 = (bf16[256,640]{1,0:T(8,128)(2,1)}, bf16[256,128,256]{2,1,0:T(8,128)(2,1)}, bf16[256,128,256]{2,1,0:T(8,128)(2,1)}, s32[256,128]{1,0:T(8,128)}) custom-call(s32[256]{0:T(256)S(1)} %copy-done, f32[256,256]{1,0:T(8,128)S(1)} %get-tuple-element.12.k_new, f32[256,256]{1,0:T(8,128)S(1)} %get-tuple-element.13.v_new, ...), custom_call_target="tpu_custom_call" | custom-call | tf_op jit(solution)/shard_map/write/pallas_call | solution.py:357
Async XLA Ops:
  0.6 29.1 %copy-start = (s32[256]{0:T(256)S(1)}, s32[256]{0:T(256)}, u32[]{:S(2)}) copy-start(s32[256]{0:T(256)} %pos.1) | copy-start | bytes 3076

commit v3 on v2

--- a/solution.py
+++ b/solution.py
@@ -26,29 +26,16 @@
 BF16 = jnp.bfloat16
 
 
-def attend_kernel(window, pos_h, freq_h, x_h, ns_h, wk_h, wv_h, wq_h, sp_h, wo_h, bo_h, k_h, v_h,
-                  *rest):
+def attend_kernel(window, pos_h, freq_h, x_h, ns_h, wk_h, wv_h, wq_h, sp_h, k_h, v_h, *rest):
     k_vm, v_vm = rest[:PIECES], rest[PIECES:2 * PIECES]
-    (x_new, k_new, v_new, sp_new,
-                  pos, freq, x_in, ns, wk, wv, wq, sp, wo, bo,
-                  pos_b, x_f, q_s, pk, rc1, cm, rc2, o_s, ag,
-                  in_sem, k_sem, v_sem, s1, r1, s2, r2, sa, ra, sb, rb, sc, rc) = rest[2 * PIECES:]
+    (pk, x_f, k_new, v_new, sp_new, pos, freq, x_in, ns, wk, wv, wq, sp, pos_b, q_s, in_sem, k_sem, v_sem) = rest[2 * PIECES:]
     me = lax.axis_index('kv')
-    x_side, core = me // 2, me % 2
-    over = {'kv': 2 * (1 - x_side) + core}
-    beside = {'kv': 2 * x_side + 1 - core}
-    over_i = 2 * (1 - x_side) + core
     batch, slots = sp.shape
     chunk = UNIT * CHUNK_UNITS
     chunks = batch // chunk
-    half = chunks // 2
-
-    barrier = pltpu.get_barrier_semaphore()
-    pl.semaphore_signal(barrier, inc=1, device_id=over, device_id_type=MESH)
-    pl.semaphore_signal(barrier, inc=1, device_id=beside, device_id_type=MESH)
 
     smalls = [pltpu.make_async_copy(src, dst, in_sem.at[n]) for n, (src, dst) in enumerate((
-        (pos_h, pos), (freq_h, freq), (x_h, x_in), (ns_h, ns), (wk_h, wk), (wv_h, wv), (wq_h, wq), (sp_h, sp), (wo_h, wo), (bo_h, bo)))]
+        (pos_h, pos), (freq_h, freq), (x_h, x_in), (ns_h, ns), (wk_h, wk), (wv_h, wv), (wq_h, wq), (sp_h, sp)))]
 
     span = chunks // PIECES
 
@@ -62,7 +49,7 @@
             for copy in cache_copy(j, j // span):
                 copy.start()
 
-    for small in smalls[:8]:
+    for small in smalls:
         small.start()
     read_ahead(0, AHEAD)
 
@@ -95,14 +82,11 @@
     v_new[...] = jnp.dot(normed, wv[...], preferred_element_type=F32).astype(BF16).astype(F32)
     smalls[6].wait()
     read_ahead(AHEAD + 1, chunks)
-    for small in smalls[8:]:
-        small.start()
     for h in range(HEADS):
         q_row = jnp.dot(normed, wq[:, h * HEAD_DIM:(h + 1) * HEAD_DIM], preferred_element_type=F32)
         q_s[:, h, :, :128] = rotate(q_row[:, :128]).reshape(batch // UNIT, UNIT, 128)
         q_s[:, h, :, 128:] = q_row[:, 128:].reshape(batch // UNIT, UNIT, 128)
     smalls[7].wait()
-    pl.semaphore_wait(barrier, 2)
 
     lane = lax.broadcasted_iota(jnp.int32, (UNIT, 128), 1)
     row_seq = lax.broadcasted_iota(jnp.int32, (ROWS, 128), 0) % UNIT
@@ -155,6 +139,33 @@
                 tile = jnp.where(lane == h, top[h], jnp.where(lane == HEADS + h, total[h], tile))
             pk[j, i, 2 * ROWS:, :] = tile
 
+    def step(piece, j, carry):
+        for copy in cache_copy(j, piece):
+            copy.wait()
+        attend(j, piece)
+        return carry
+
+    for piece in range(PIECES):
+        lax.fori_loop(piece * span, (piece + 1) * span, functools.partial(step, piece), 0)
+
+
+def exchange_kernel(wo_h, bo_h, pk, x_f, x_new, wo, bo, rc1, cm, rc2, o_s, ag, in_sem, s1, r1, s2, r2, sa, ra, sb, rb, sc, rc):
+    me = lax.axis_index('kv')
+    x_side, core = me // 2, me % 2
+    over_i = 2 * (1 - x_side) + core
+    over = {'kv': over_i}
+    beside = {'kv': 2 * x_side + 1 - core}
+    chunks = pk.shape[0]
+    chunk = UNIT * CHUNK_UNITS
+    half = chunks // 2
+    barrier = pltpu.get_barrier_semaphore()
+    pl.semaphore_signal(barrier, inc=1, device_id=over, device_id_type=MESH)
+    pl.semaphore_signal(barrier, inc=1, device_id=beside, device_id_type=MESH)
+    smalls = [pltpu.make_async_copy(src, dst, in_sem.at[n]) for n, (src, dst) in enumerate(((wo_h, wo), (bo_h, bo)))]
+    for small in smalls:
+        small.start()
+    lane = lax.broadcasted_iota(jnp.int32, (UNIT, 128), 1)
+
     def merge(a, b):
         ta, tb = a[2 * ROWS:, :], b[2 * ROWS:, :]
         tile = jnp.maximum(ta, tb)
@@ -209,36 +220,29 @@
         gather_copy(g, me, over, sa, ra).wait_recv()
         gather_copy(g, over_i, beside, sc, rc).start()
 
-    def step(piece, j, carry):
-        for copy in cache_copy(j, piece):
-            copy.wait()
-        attend(j, piece)
+    pl.semaphore_wait(barrier, 2)
+
+    def send(j, carry):
         first_copy(j).start()
-
-        @pl.when(j >= 1)
-        def _():
-            first_merge(j - 1)
-
-        @pl.when(j >= 3)
-        def _():
-            second_merge(j - 3)
-
-        @pl.when(j == half + 2)
-        def _():
-            smalls[8].wait()
-            smalls[9].wait()
-            project(0)
-
-        return carry
-
-    for piece in range(PIECES):
-        lax.fori_loop(piece * span, (piece + 1) * span, functools.partial(step, piece), 0)
-    second_merge(chunks - 3)
+        return carry
+
+    def first(j, carry):
+        first_merge(j)
+        return carry
+
+    def second(j, carry):
+        second_merge(j)
+        return carry
+
+    lax.fori_loop(0, chunks, send, 0)
+    lax.fori_loop(0, chunks, first, 0)
+    for small in smalls:
+        small.wait()
+    lax.fori_loop(0, half, second, 0)
+    project(0)
+    lax.fori_loop(half, chunks, second, 0)
+    project(1)
     forward(0)
-    first_merge(chunks - 1)
-    second_merge(chunks - 2)
-    second_merge(chunks - 1)
-    project(1)
     forward(1)
     for g in range(2):
         gather_copy(g, me, beside, sb, rb).wait_recv()
@@ -334,26 +338,36 @@
         smem = pl.BlockSpec(memory_space=pltpu.SMEM)
         dma = pltpu.SemaphoreType.DMA
         per_chunk = [dma((chunks,))] * 4
-        *held, x_new, k_new, v_new, sp_new = pl.pallas_call(
+        at_hbm = functools.partial(pltpu.with_memory_space_constraint, memory_space=pltpu.HBM)
+        *held, pk, x_f, k_new, v_new, sp_new = pl.pallas_call(
             functools.partial(attend_kernel, window),
-            out_shape=(*([pltpu.VMEM((batch // PIECES, slots, HEAD_DIM), BF16)] * (2 * PIECES)), pltpu.VMEM((batch, model), BF16),
+            out_shape=(*([pltpu.VMEM((batch // PIECES, slots, HEAD_DIM), BF16)] * (2 * PIECES)),
+                       pltpu.VMEM((chunks, CHUNK_UNITS, PACKET, 128), F32), pltpu.VMEM((batch, model), F32),
                        pltpu.VMEM((batch, HEAD_DIM), F32), pltpu.VMEM((batch, HEAD_DIM), F32), pltpu.VMEM((batch, slots), jnp.int32)),
-            in_specs=[hbm] * 12,
-            out_specs=(vmem,) * (2 * PIECES + 4),
+            in_specs=[hbm] * 10,
+            out_specs=(vmem,) * (2 * PIECES + 5),
             scratch_shapes=[
                 pltpu.VMEM((batch // 128, 128), jnp.int32), pltpu.VMEM((1, 128), F32), pltpu.VMEM((batch, model), BF16), pltpu.VMEM((model,), BF16),
                 pltpu.VMEM((model, HEAD_DIM), BF16), pltpu.VMEM((model, HEAD_DIM), BF16), pltpu.VMEM((model, width), BF16),
-                pltpu.VMEM((batch, slots), jnp.int32), pltpu.VMEM((width, model), BF16), pltpu.VMEM((model,), BF16),
-                pltpu.VMEM((batch, 128), F32), pltpu.VMEM((batch, model), F32), pltpu.VMEM((batch // UNIT, HEADS, UNIT, HEAD_DIM), F32),
-                pltpu.VMEM((chunks, CHUNK_UNITS, PACKET, 128), F32), pltpu.VMEM((chunks, 2, PACKET, 128), F32),
+                pltpu.VMEM((batch, slots), jnp.int32),
+                pltpu.VMEM((batch, 128), F32), pltpu.VMEM((batch // UNIT, HEADS, UNIT, HEAD_DIM), F32),
+                dma((8,)), dma((chunks,)), dma((chunks,))],
+            compiler_params=pltpu.CompilerParams(vmem_limit_bytes=14 << 20),
+            name='attend',
+        )(*map(at_hbm, (positions.reshape(batch // 128, 128), jnp.asarray(freq_row), x_in, norm_scale, w_k, w_v, w_q, slot_pos, k_cache, v_cache)))
+        x_new = pl.pallas_call(
+            exchange_kernel,
+            out_shape=pltpu.VMEM((batch, model), BF16),
+            in_specs=[hbm] * 2 + [vmem] * 2,
+            out_specs=vmem,
+            scratch_shapes=[
+                pltpu.VMEM((width, model), BF16), pltpu.VMEM((model,), BF16), pltpu.VMEM((chunks, 2, PACKET, 128), F32),
                 pltpu.VMEM((chunks, 2, PACKET, 128), F32), pltpu.VMEM((chunks, PACKET, 128), F32),
                 pltpu.VMEM((chunks * UNIT, width), F32), pltpu.VMEM((kv_size, chunks * UNIT, model), F32),
-                dma((10,)), dma((chunks,)), dma((chunks,)), *per_chunk, *([dma((2,))] * 6)],
-            compiler_params=pltpu.CompilerParams(vmem_limit_bytes=16 << 20, collective_id=0, has_side_effects=True),
-            name='attend',
-        )(*[pltpu.with_memory_space_constraint(a, pltpu.HBM) for a in (
-            positions.reshape(batch // 128, 128), jnp.asarray(freq_row), x_in, norm_scale, w_k, w_v, w_q, slot_pos,
-            w_o, b_o, k_cache, v_cache)])
+                dma((2,)), *per_chunk, *([dma((2,))] * 6)],
+            compiler_params=pltpu.CompilerParams(vmem_limit_bytes=10 << 20, collective_id=0, has_side_effects=True),
+            name='exchange',
+        )(at_hbm(w_o), at_hbm(b_o), pk, x_f)
         x_out, k_out, v_out, slot_pos_out = pl.pallas_call(
             functools.partial(write_kernel, window),
             out_shape=(jax.ShapeDtypeStruct((batch, model), BF16), jax.ShapeDtypeStruct(k_cache.shape, BF16),

time: 41.6 us -> 44.1 us (1.060)
  Pallas kernels: 40.9 us -> 43.3 us
    pallas_call x0 -> x1, Pallas kernels: none -> 18.3 us  [local_step(): pl.pallas_call(exchange_kernel, out_shape=pltpu.VMEM((batch, model), BF16...]
    pallas_call x1, Pallas kernels: 29.1 us -> 13.2 us  [local_step(): pl.pallas_call(functools.partial(attend_kernel, window), out_shape=(*[plt...]
where the time goes in v3:
time: 44.1 us; the launch traced here: 44 us
  Pallas kernels  43.3 us (98%)
  between operations  0.67 us (2%)
    pallas_call x1, Pallas kernels, local_step(): pl.pallas_call(exchange_kernel, out_shape=pltpu.VMEM((batch, model), BF16...  18.3 us
    pallas_call x1, Pallas kernels, local_step(): pl.pallas_call(functools.partial(attend_kernel, window), out_shape=(*[plt...  13.2 us
    pallas_call x1, Pallas kernels, local_step(): pl.pallas_call(functools.partial(write_kernel, window), out_shape=(jax.Sh...  11.8 us

profile of v3, /device:TPU:0, one launch (start us, length us, event | category | flops | bytes accessed | tf_op | source)
XLA Modules:
  0.0 44.0 jit_solution(10585152673826868005)
XLA Ops:
  0.6 0.0 copy-start
  0.6 13.2 %attend.1 = (bf16[128,128,256]{2,1,0:T(8,128)(2,1)S(1)}, bf16[128,128,256]{2,1,0:T(8,128)(2,1)S(1)}, bf16[128,128,256]{2,1,0:T(8,128)(2,1)S(1)}, bf16[128,128,25...) custom-call(s32[2,128]{1,0:T(2,128)} %bitcast.1, ...), custom_call_target="tpu_custom_call" | custom-call | tf_op jit(solution)/shard_map/attend/pallas_call | solution.py:342
  13.9 18.3 %exchange.1.x_new = bf16[256,640]{1,0:T(8,128)(2,1)S(1)} custom-call(bf16[1024,640]{1,0:T(8,128)(2,1)} %wo_h.1, bf16[640]{0:T(1024)(128)(2,1)} %bo_h.1, f32[8,4,72,128]{3,2,1,0:T(8,128)S(1)} %get-tuple-element.15.pk, f32[256,640]{1,0:T(8,128)S(1)} %get-tuple-element.16.x_f), custom_call_target="tpu_custom_call" | custom-call | tf_op jit(solution)/shard_map/exchange/pallas_call | solution.py:358
  32.2 0.0 copy-done
  32.2 11.8 %write.1 = (bf16[256,640]{1,0:T(8,128)(2,1)}, bf16[256,128,256]{2,1,0:T(8,128)(2,1)}, bf16[256,128,256]{2,1,0:T(8,128)(2,1)}, s32[256,128]{1,0:T(8,128)}) custom-call(s32[256]{0:T(256)S(1)} %copy-done, f32[256,256]{1,0:T(8,128)S(1)} %get-tuple-element.13.k_new, f32[256,256]{1,0:T(8,128)S(1)} %get-tuple-element.14.v_new, bf16[256,640]{1,0:T(8,128)(2,1)S(1)} %exchange.1.x_new, ...), custom_call_target="tpu_custom_call" | custom-call | tf_op jit(solution)/shard_map/write/pallas_call | solution.py:371
Async XLA Ops:
  0.6 31.5 %copy-start = (s32[256]{0:T(256)S(1)}, s32[256]{0:T(256)}, u32[]{:S(2)}) copy-start(s32[256]{0:T(256)} %pos.1) | copy-start | bytes 3076

commit v4 on v2

--- a/solution.py
+++ b/solution.py
@@ -20,7 +20,7 @@
 ROWS = UNIT * HEADS
 PACKET = 2 * ROWS + 8
 PIECES = 2
-AHEAD = 3
+AHEAD = 2
 MESH = pl.DeviceIdType.MESH
 F32 = jnp.float32
 BF16 = jnp.bfloat16
@@ -80,7 +80,6 @@
     def rotate(first):
         return first * cos_t + pltpu.roll(first, ROPE_DIM // 2, 1) * sin_t
 
-    read_ahead(AHEAD, AHEAD + 1)
     smalls[2].wait()
     smalls[3].wait()
     x32 = x_in[...].astype(F32)
@@ -94,7 +93,6 @@
     k_new[:, 128:] = k_row[:, 128:].astype(BF16).astype(F32)
     v_new[...] = jnp.dot(normed, wv[...], preferred_element_type=F32).astype(BF16).astype(F32)
     smalls[6].wait()
-    read_ahead(AHEAD + 1, chunks)
     for small in smalls[8:]:
         small.start()
     for h in range(HEADS):
@@ -228,6 +226,12 @@
             smalls[8].wait()
             smalls[9].wait()
             project(0)
+
+        for ahead in range(PIECES):
+            @pl.when((j + AHEAD < chunks) & ((j + AHEAD) // span == ahead))
+            def _():
+                for copy in cache_copy(j + AHEAD, ahead):
+                    copy.start()
 
         return carry
 

time: 41.6 us -> 43.1 us (1.036)
  Pallas kernels: 40.9 us -> 42.3 us
    pallas_call x1, Pallas kernels: 29.1 us -> 30.5 us  [local_step(): pl.pallas_call(functools.partial(attend_kernel, window), out_shape=(*[plt...]
where the time goes in v4:
time: 43.1 us; the launch traced here: 43 us
  Pallas kernels  42.3 us (98%)
  between operations  0.66 us (2%)
    pallas_call x1, Pallas kernels, local_step(): pl.pallas_call(functools.partial(attend_kernel, window), out_shape=(*[plt...  30.5 us
    pallas_call x1, Pallas kernels, local_step(): pl.pallas_call(functools.partial(write_kernel, window), out_shape=(jax.Sh...  11.8 us

profile of v4, /device:TPU:0, one launch (start us, length us, event | category | flops | bytes accessed | tf_op | source)
XLA Modules:
  0.0 43.0 jit_solution(5038321600057736160)
XLA Ops:
  0.6 0.0 copy-start
  0.6 30.5 %attend.1 = (bf16[128,128,256]{2,1,0:T(8,128)(2,1)S(1)}, bf16[128,128,256]{2,1,0:T(8,128)(2,1)S(1)}, bf16[128,128,256]{2,1,0:T(8,128)(2,1)S(1)}, bf16[128,128,25...) custom-call(s32[2,128]{1,0:T(2,128)} %bitcast.1, ...), custom_call_target="tpu_custom_call" | custom-call | tf_op jit(solution)/shard_map/attend/pallas_call | solution.py:341
  31.2 0.0 copy-done
  31.2 11.8 %write.1 = (bf16[256,640]{1,0:T(8,128)(2,1)}, bf16[256,128,256]{2,1,0:T(8,128)(2,1)}, bf16[256,128,256]{2,1,0:T(8,128)(2,1)}, s32[256,128]{1,0:T(8,128)}) custom-call(s32[256]{0:T(256)S(1)} %copy-done, f32[256,256]{1,0:T(8,128)S(1)} %get-tuple-element.12.k_new, f32[256,256]{1,0:T(8,128)S(1)} %get-tuple-element.13.v_new, ...), custom_call_target="tpu_custom_call" | custom-call | tf_op jit(solution)/shard_map/write/pallas_call | solution.py:361
Async XLA Ops:
  0.6 30.5 %copy-start = (s32[256]{0:T(256)S(1)}, s32[256]{0:T(256)}, u32[]{:S(2)}) copy-start(s32[256]{0:T(256)} %pos.1) | copy-start | bytes 3076

commit v5 on v4

--- a/solution.py
+++ b/solution.py
@@ -20,6 +20,9 @@
 ROWS = UNIT * HEADS
 PACKET = 2 * ROWS + 8
 PIECES = 2
+FIRST_LAG = 2
+SECOND_LAG = 5
+RING = 4
 AHEAD = 2
 MESH = pl.DeviceIdType.MESH
 F32 = jnp.float32
@@ -29,19 +32,17 @@
 def attend_kernel(window, pos_h, freq_h, x_h, ns_h, wk_h, wv_h, wq_h, sp_h, wo_h, bo_h, k_h, v_h,
                   *rest):
     k_vm, v_vm = rest[:PIECES], rest[PIECES:2 * PIECES]
-    (x_new, k_new, v_new, sp_new,
+    (x_own, k_new, v_new, sp_new,
                   pos, freq, x_in, ns, wk, wv, wq, sp, wo, bo,
-                  pos_b, x_f, q_s, pk, rc1, cm, rc2, o_s, ag,
-                  in_sem, k_sem, v_sem, s1, r1, s2, r2, sa, ra, sb, rb, sc, rc) = rest[2 * PIECES:]
+                  pos_b, x_f, q_s, pk, rc1, cm, rc2, o_s,
+                  in_sem, k_sem, v_sem, s1, r1, s2, r2) = rest[2 * PIECES:]
     me = lax.axis_index('kv')
     x_side, core = me // 2, me % 2
     over = {'kv': 2 * (1 - x_side) + core}
     beside = {'kv': 2 * x_side + 1 - core}
-    over_i = 2 * (1 - x_side) + core
     batch, slots = sp.shape
     chunk = UNIT * CHUNK_UNITS
     chunks = batch // chunk
-    half = chunks // 2
 
     barrier = pltpu.get_barrier_semaphore()
     pl.semaphore_signal(barrier, inc=1, device_id=over, device_id_type=MESH)
@@ -192,20 +193,10 @@
 
     own_unit = 2 * core + x_side
 
-    def gather_copy(g, owner, target, send, recv):
-        rows = ag.at[owner, pl.ds(g * half * UNIT, half * UNIT)]
-        return pltpu.make_async_remote_copy(rows, rows, send.at[g], recv.at[g], device_id=target, device_id_type=MESH)
-
-    def project(g):
-        o_b = o_s[pl.ds(g * half * UNIT, half * UNIT), :].astype(BF16)
-        rows = jnp.concatenate([x_f[pl.ds((g * half + i) * chunk + own_unit * UNIT, UNIT), :] for i in range(half)], axis=0)
-        ag[me, pl.ds(g * half * UNIT, half * UNIT), :] = rows + jnp.dot(o_b, wo[...], preferred_element_type=F32) + bo[...].astype(F32)[None, :]
-        gather_copy(g, me, over, sa, ra).start()
-        gather_copy(g, me, beside, sb, rb).start()
-
-    def forward(g):
-        gather_copy(g, me, over, sa, ra).wait_recv()
-        gather_copy(g, over_i, beside, sc, rc).start()
+    def project(first, last):
+        rows = pl.ds(first * UNIT, (last - first) * UNIT)
+        residual = jnp.concatenate([x_f[pl.ds(j * chunk + own_unit * UNIT, UNIT), :] for j in range(first, last)], axis=0)
+        x_own[rows, :] = residual + jnp.dot(o_s[rows, :].astype(BF16), wo[...], preferred_element_type=F32) + bo[...].astype(F32)[None, :]
 
     def step(piece, j, carry):
         for copy in cache_copy(j, piece):
@@ -213,19 +204,13 @@
         attend(j, piece)
         first_copy(j).start()
 
-        @pl.when(j >= 1)
+        @pl.when(j >= FIRST_LAG)
         def _():
-            first_merge(j - 1)
-
-        @pl.when(j >= 3)
+            first_merge(j - FIRST_LAG)
+
+        @pl.when(j >= SECOND_LAG)
         def _():
-            second_merge(j - 3)
-
-        @pl.when(j == half + 2)
-        def _():
-            smalls[8].wait()
-            smalls[9].wait()
-            project(0)
+            second_merge(j - SECOND_LAG)
 
         for ahead in range(PIECES):
             @pl.when((j + AHEAD < chunks) & ((j + AHEAD) // span == ahead))
@@ -237,20 +222,16 @@
 
     for piece in range(PIECES):
         lax.fori_loop(piece * span, (piece + 1) * span, functools.partial(step, piece), 0)
-    second_merge(chunks - 3)
-    forward(0)
-    first_merge(chunks - 1)
-    second_merge(chunks - 2)
-    second_merge(chunks - 1)
-    project(1)
-    forward(1)
-    for g in range(2):
-        gather_copy(g, me, beside, sb, rb).wait_recv()
-        gather_copy(g, me, beside, sc, rc).wait_recv()
-    for c in range(2):
-        for j in range(chunks):
-            rows = [ag[2 * s + c, j * UNIT:(j + 1) * UNIT, :] for s in range(2)]
-            x_new[j * chunk + 2 * UNIT * c:j * chunk + 2 * UNIT * (c + 1), :] = jnp.concatenate(rows, axis=0).astype(BF16)
+    for j in range(chunks - FIRST_LAG, chunks):
+        first_merge(j)
+    for small in smalls[8:]:
+        small.wait()
+    for j in range(chunks - SECOND_LAG, chunks - FIRST_LAG):
+        second_merge(j)
+    project(0, chunks - FIRST_LAG)
+    for j in range(chunks - FIRST_LAG, chunks):
+        second_merge(j)
+    project(chunks - FIRST_LAG, chunks)
 
     def drain(j, carry):
         first_copy(j).wait_send()
@@ -258,38 +239,25 @@
         return carry
 
     lax.fori_loop(0, chunks, drain, 0)
-    for g in range(2):
-        gather_copy(g, me, over, sa, ra).wait_send()
-        gather_copy(g, me, beside, sb, rb).wait_send()
-        gather_copy(g, over_i, beside, sc, rc).wait_send()
-
-
-def write_kernel(window, pos, k_new, v_new, x_new, sp_new, *rest):
-    k_vm, v_vm = rest[:PIECES], rest[PIECES:2 * PIECES]
-    x_out, k_out, v_out, sp_out, k_ring, v_ring, sems, k_sem, v_sem = rest[2 * PIECES:]
+
+
+def insert_rows(window, pos, new, held, out, ring, sem):
     me = lax.axis_index('kv')
-    part, slots, _ = k_vm[0].shape
-    batch = part * PIECES
-    depth, chunk = k_ring.shape[:2]
-    chunks = batch // chunk
-    span = chunks // PIECES
-    others = (pltpu.make_async_copy(x_new, x_out, sems.at[0]), pltpu.make_async_copy(sp_new, sp_out, sems.at[1]))
-    for copy in others:
-        copy.start()
+    part, slots, _ = held[0].shape
+    depth, chunk = ring.shape[:2]
+    span = part // chunk
     tile_row = lax.broadcasted_iota(jnp.int32, (16, HEAD_DIM), 0)
 
-    def copies(j):
-        rows, ring = pl.ds(j * chunk, chunk), lax.rem(j, depth)
-        return (pltpu.make_async_copy(k_ring.at[ring], k_out.at[rows], k_sem.at[ring]),
-                pltpu.make_async_copy(v_ring.at[ring], v_out.at[rows], v_sem.at[ring]))
+    def copy_out(j):
+        turn = lax.rem(j, depth)
+        return pltpu.make_async_copy(ring.at[turn], out.at[pl.ds(j * chunk, chunk)], sem.at[turn])
 
     def step(piece, j, carry):
-        ring = lax.rem(j, depth)
+        turn = lax.rem(j, depth)
 
         @pl.when(j >= depth)
         def _():
-            for copy in copies(j - depth):
-                copy.wait()
+            copy_out(j - depth).wait()
 
         def group(i, carry):
             for n in range(8):
@@ -297,24 +265,44 @@
                 b = j * chunk + row
                 slot = (pos[b] & (window - 1)) - me * slots
                 base = pl.multiple_of((jnp.clip(slot, 0, slots - 1) // 16) * 16, 16)
-                for new, cache, out in ((k_new, k_vm[piece], k_ring), (v_new, v_vm[piece], v_ring)):
-                    out[ring, row] = cache[b - piece * part]
-                    fresh = jnp.broadcast_to(new[pl.ds(b, 1), :], (16, HEAD_DIM))
-                    old = cache[b - piece * part, pl.ds(base, 16), :].astype(F32)
-                    out[ring, row, pl.ds(base, 16), :] = jnp.where(tile_row == slot - base, fresh, old).astype(BF16)
+                ring[turn, row] = held[piece][b - piece * part]
+                fresh = jnp.broadcast_to(new[pl.ds(b, 1), :], (16, HEAD_DIM))
+                old = held[piece][b - piece * part, pl.ds(base, 16), :].astype(F32)
+                ring[turn, row, pl.ds(base, 16), :] = jnp.where(tile_row == slot - base, fresh, old).astype(BF16)
             return carry
         lax.fori_loop(0, chunk // 8, group, 0)
-        for copy in copies(j):
-            copy.start()
+        copy_out(j).start()
         return carry
 
     for piece in range(PIECES):
         lax.fori_loop(piece * span, (piece + 1) * span, functools.partial(step, piece), 0)
-    for j in range(chunks - depth, chunks):
-        for copy in copies(j):
-            copy.wait()
-    for copy in others:
-        copy.wait()
+    for j in range(PIECES * span - depth, PIECES * span):
+        copy_out(j).wait()
+
+
+def write_keys_kernel(window, pos, k_new, sp_new, *rest):
+    held = rest[:PIECES]
+    k_out, sp_out, ring, sem, sp_sem = rest[PIECES:]
+    copy = pltpu.make_async_copy(sp_new, sp_out, sp_sem)
+    copy.start()
+    insert_rows(window, pos, k_new, held, k_out, ring, sem)
+    copy.wait()
+
+
+def write_values_kernel(window, pos, v_new, x_own, x_beside, x_over, x_across, *rest):
+    held = rest[:PIECES]
+    v_out, x_out, ring, x_rows, x_new, sem, x_sem = rest[PIECES:]
+    me = lax.axis_index('kv')
+    for flip, rows in enumerate((x_own, x_beside, x_over, x_across)):
+        x_side, core = (me // 2 + flip // 2) % 2, (me % 2 + flip % 2) % 2
+        unit = 2 * core + x_side
+        for j in range(rows.shape[0] // UNIT):
+            x_rows[pl.ds(j * UNIT * CHUNK_UNITS + unit * UNIT, UNIT), :] = rows[j * UNIT:(j + 1) * UNIT, :]
+    x_new[...] = x_rows[...].astype(BF16)
+    copy = pltpu.make_async_copy(x_new, x_out, x_sem)
+    copy.start()
+    insert_rows(window, pos, v_new, held, v_out, ring, sem)
+    copy.wait()
 
 
 def solution(mesh):
@@ -338,9 +326,9 @@
         smem = pl.BlockSpec(memory_space=pltpu.SMEM)
         dma = pltpu.SemaphoreType.DMA
         per_chunk = [dma((chunks,))] * 4
-        *held, x_new, k_new, v_new, sp_new = pl.pallas_call(
+        *held, x_own, k_new, v_new, sp_new = pl.pallas_call(
             functools.partial(attend_kernel, window),
-            out_shape=(*([pltpu.VMEM((batch // PIECES, slots, HEAD_DIM), BF16)] * (2 * PIECES)), pltpu.VMEM((batch, model), BF16),
+            out_shape=(*([pltpu.VMEM((batch // PIECES, slots, HEAD_DIM), BF16)] * (2 * PIECES)), pltpu.VMEM((chunks * UNIT, model), F32),
                        pltpu.VMEM((batch, HEAD_DIM), F32), pltpu.VMEM((batch, HEAD_DIM), F32), pltpu.VMEM((batch, slots), jnp.int32)),
             in_specs=[hbm] * 12,
             out_specs=(vmem,) * (2 * PIECES + 4),
@@ -351,23 +339,35 @@
                 pltpu.VMEM((batch, 128), F32), pltpu.VMEM((batch, model), F32), pltpu.VMEM((batch // UNIT, HEADS, UNIT, HEAD_DIM), F32),
                 pltpu.VMEM((chunks, CHUNK_UNITS, PACKET, 128), F32), pltpu.VMEM((chunks, 2, PACKET, 128), F32),
                 pltpu.VMEM((chunks, 2, PACKET, 128), F32), pltpu.VMEM((chunks, PACKET, 128), F32),
-                pltpu.VMEM((chunks * UNIT, width), F32), pltpu.VMEM((kv_size, chunks * UNIT, model), F32),
-                dma((10,)), dma((chunks,)), dma((chunks,)), *per_chunk, *([dma((2,))] * 6)],
+                pltpu.VMEM((chunks * UNIT, width), F32),
+                dma((10,)), dma((chunks,)), dma((chunks,)), *per_chunk],
             compiler_params=pltpu.CompilerParams(vmem_limit_bytes=16 << 20, collective_id=0, has_side_effects=True),
             name='attend',
         )(*[pltpu.with_memory_space_constraint(a, pltpu.HBM) for a in (
             positions.reshape(batch // 128, 128), jnp.asarray(freq_row), x_in, norm_scale, w_k, w_v, w_q, slot_pos,
             w_o, b_o, k_cache, v_cache)])
-        x_out, k_out, v_out, slot_pos_out = pl.pallas_call(
-            functools.partial(write_kernel, window),
-            out_shape=(jax.ShapeDtypeStruct((batch, model), BF16), jax.ShapeDtypeStruct(k_cache.shape, BF16),
-                       jax.ShapeDtypeStruct(v_cache.shape, BF16), jax.ShapeDtypeStruct((batch, slots), jnp.int32)),
-            in_specs=[smem] + [vmem] * (2 * PIECES + 4),
-            out_specs=(hbm,) * 4,
-            scratch_shapes=[pltpu.VMEM((4, 16, slots, HEAD_DIM), BF16), pltpu.VMEM((4, 16, slots, HEAD_DIM), BF16), dma((2,)), dma((4,)), dma((4,))],
-            compiler_params=pltpu.CompilerParams(vmem_limit_bytes=9 << 20),
-            name='write',
-        )(positions, k_new, v_new, x_new, sp_new, *held)
+        x_beside, x_over, x_across = [lax.ppermute(x_own, 'kv', [(i, i ^ flip) for i in range(kv_size)]) for flip in range(1, kv_size)]
+        traffic = pl.CostEstimate(flops=0, bytes_accessed=k_cache.size * 2, transcendentals=0)
+        k_out, slot_pos_out = pl.pallas_call(
+            functools.partial(write_keys_kernel, window),
+            out_shape=(jax.ShapeDtypeStruct(k_cache.shape, BF16), jax.ShapeDtypeStruct((batch, slots), jnp.int32)),
+            in_specs=[smem] + [vmem] * (PIECES + 2),
+            out_specs=(hbm,) * 2,
+            scratch_shapes=[pltpu.VMEM((RING, 16, slots, HEAD_DIM), BF16), dma((RING,)), dma],
+            compiler_params=pltpu.CompilerParams(vmem_limit_bytes=7 << 20),
+            cost_estimate=traffic,
+            name='write_keys',
+        )(positions, k_new, sp_new, *held[:PIECES])
+        v_out, x_out = pl.pallas_call(
+            functools.partial(write_values_kernel, window),
+            out_shape=(jax.ShapeDtypeStruct(v_cache.shape, BF16), jax.ShapeDtypeStruct((batch, model), BF16)),
+            in_specs=[smem] + [vmem] * (PIECES + 5),
+            out_specs=(hbm,) * 2,
+            scratch_shapes=[pltpu.VMEM((RING, 16, slots, HEAD_DIM), BF16), pltpu.VMEM((batch, model), F32), pltpu.VMEM((batch, model), BF16), dma((RING,)), dma],
+            compiler_params=pltpu.CompilerParams(vmem_limit_bytes=7 << 20),
+            cost_estimate=traffic,
+            name='write_values',
+        )(positions, v_new, x_own, x_beside, x_over, x_across, *held[PIECES:])
         return x_out, k_out, v_out, slot_pos_out
 
     return jax.shard_map(

time: 43.1 us -> 41.4 us (0.961)
  Pallas kernels: 42.3 us -> 37.2 us
  starting transfers between devices: 0 us -> 1.89 us
  waiting for transfers between devices: 0 us -> 1.52 us
    pallas_call x1, Pallas kernels: 30.5 us -> 23.8 us  [local_step(): pl.pallas_call(functools.partial(attend_kernel, window), out_shape=(*[plt...]
    ppermute x0 -> x3, starting transfers between devices: none -> 1.89 us  [local_step(): lax.ppermute(x_own, 'kv', [(i, i ^ flip) for i in range(kv_size)])]
    pallas_call x1 -> x2, Pallas kernels: 11.8 us -> 13.3 us  [the longest x1 6.71 us: local_step(): pl.pallas_call(functools.partial(write_values_kernel, window), out_shape=...]
    ppermute x0 -> x3, waiting for transfers between devices: none -> 1.52 us  [local_step(): lax.ppermute(x_own, 'kv', [(i, i ^ flip) for i in range(kv_size)])]
  transfers between devices with their start and end apart: 0 -> 3, of which waited for: 0 -> 1; matrix products, arithmetic and copies ran while one was open for 0% -> 0% of each run, Pallas kernels for 0% -> 16%
where the time goes in v5:
time: 41.4 us; the launch traced here: 41.3 us
  Pallas kernels  37.2 us (90%)
  starting transfers between devices  1.89 us (5%)
  waiting for transfers between devices  1.52 us (4%)
  between operations  0.68 us (2%)
    pallas_call x1, Pallas kernels, local_step(): pl.pallas_call(functools.partial(attend_kernel, window), out_shape=(*[plt...  23.8 us
    pallas_call x1, Pallas kernels, local_step(): pl.pallas_call(functools.partial(write_values_kernel, window), out_shape=...  6.71 us
    pallas_call x1, Pallas kernels, local_step(): pl.pallas_call(functools.partial(write_keys_kernel, window), out_shape=(j...  6.61 us
    ppermute x3, starting transfers between devices, local_step(): lax.ppermute(x_own, 'kv', [(i, i ^ flip) for i in range(kv_size)])  1.89 us
    ppermute x3, waiting for transfers between devices, local_step(): lax.ppermute(x_own, 'kv', [(i, i ^ flip) for i in range(kv_size)])  1.52 us
  transfers between devices with their start and end apart: 3, of which 1 were waited for; matrix products, arithmetic and copies ran while one was open for 0% of the time, Pallas kernels for 16%

profile of v5, /device:TPU:0, one launch (start us, length us, event | category | flops | bytes accessed | tf_op | source)
XLA Modules:
  0.0 41.3 jit_solution(11268528226425914428)
XLA Ops:
  0.6 0.0 copy-start
  0.6 23.8 %attend.1 = (bf16[128,128,256]{2,1,0:T(8,128)(2,1)S(1)}, bf16[128,128,256]{2,1,0:T(8,128)(2,1)S(1)}, bf16[128,128,256]{2,1,0:T(8,128)(2,1)S(1)}, bf16[128,128,25...) custom-call(s32[2,128]{1,0:T(2,128)} %bitcast.1, ...), custom_call_target="tpu_custom_call" | custom-call | tf_op jit(solution)/shard_map/attend/pallas_call | solution.py:329
  24.5 0.0 collective-permute-start.2
  24.5 1.5 %collective-permute-start.1 = (f32[64,640]{1,0:T(8,128)S(1)}, f32[64,640]{1,0:T(8,128)S(1)}, u32[]{:S(2)}, u32[]{:S(2)}) collective-permute-start(f32[64,640]{1,0:T(8,128)S(1)} %get-tuple-element.17.x_own), channel_id=1, source_target_pairs={{0,2},{1,3},{2,0},{3,1},{4,6},{5,7},{6,4},{7,5},{8,10},{9,11},{10,... | collective-permute-start | bytes 491528 | tf_op jit(solution)/shard_map/ppermute | solution.py:349
  26.1 0.3 collective-permute-start
  26.4 0.0 copy-done
  26.4 6.6 %write_keys.1 = (bf16[256,128,256]{2,1,0:T(8,128)(2,1)}, s32[256,128]{1,0:T(8,128)}) custom-call(s32[256]{0:T(256)S(1)} %copy-done, f32[256,256]{1,0:T(8,128)S(1)} %get-tuple-element.21.k_new, s32[256,128]{1,0:T(8,128)S(1)} %get-tuple-element.22.sp_new, bf16[128,128,256]{2,1,0:T(8,128)(2,1)S(1)} %get-tuple-element.23.rest_0_, ...), custom_call_target="tpu_custom_call" | custom-call | bytes 16777216 | tf_op jit(solution)/shard_map/write_keys/pallas_call | solution.py:351
  33.0 0.0 collective-permute-done.2.x_across
  33.0 1.5 %collective-permute-done.1.x_over = f32[64,640]{1,0:T(8,128)S(1)} collective-permute-done((f32[64,640]{1,0:T(8,128)S(1)}, f32[64,640]{1,0:T(8,128)S(1)}, u32[]{:S(2)}, u32[]{:S(2)}) %collective-permute-start.1) | collective-permute-done | bytes 163872 | tf_op jit(solution)/shard_map/ppermute | solution.py:349
  34.5 0.0 collective-permute-done.x_beside
  34.5 6.7 %write_values.1 = (bf16[256,128,256]{2,1,0:T(8,128)(2,1)}, bf16[256,640]{1,0:T(8,128)(2,1)}) custom-call(s32[256]{0:T(256)S(1)} %copy-done, f32[256,256]{1,0:T(8,128)S(1)} %get-tuple-element.16.v_new, f32[64,640]{1,0:T(8,128)S(1)} %get-tuple-element.17.x_own, f32[64,640]{1,0:T(8,128)S(1)} %collective-permute-done.x_beside, ...), custom_call_target="tpu_custom_call" | custom-call | bytes 16777216 | tf_op jit(solution)/shard_map/write_values/pallas_call | solution.py:361
Async XLA Ops:
  0.6 25.8 %copy-start = (s32[256]{0:T(256)S(1)}, s32[256]{0:T(256)}, u32[]{:S(2)}) copy-start(s32[256]{0:T(256)} %pos.3) | copy-start | bytes 3076
  24.5 8.5 %collective-permute-start.2 = (f32[64,640]{1,0:T(8,128)S(1)}, f32[64,640]{1,0:T(8,128)S(1)}, u32[]{:S(2)}, u32[]{:S(2)}) collective-permute-start(f32[64,640]{1,0:T(8,128)S(1)} %get-tuple-element.17.x_own), channel_id=1, source_target_pairs={{0,3},{1,2},{2,1},{3,0},{4,7},{5,6},{6,5},{7,4},{8,11},{9,10},{10,... | collective-permute-start | bytes 491528 | tf_op jit(solution)/shard_map/ppermute | solution.py:349
  24.5 10.0 %collective-permute-start.1 = (f32[64,640]{1,0:T(8,128)S(1)}, f32[64,640]{1,0:T(8,128)S(1)}, u32[]{:S(2)}, u32[]{:S(2)}) collective-permute-start(f32[64,640]{1,0:T(8,128)S(1)} %get-tuple-element.17.x_own), channel_id=1, source_target_pairs={{0,2},{1,3},{2,0},{3,1},{4,6},{5,7},{6,4},{7,5},{8,10},{9,11},{10,... | collective-permute-start | bytes 491528 | tf_op jit(solution)/shard_map/ppermute | solution.py:349
  26.1 8.5 %collective-permute-start = (f32[64,640]{1,0:T(8,128)S(1)}, f32[64,640]{1,0:T(8,128)S(1)}, u32[]{:S(2)}, u32[]{:S(2)}) collective-permute-start(f32[64,640]{1,0:T(8,128)S(1)} %get-tuple-element.17.x_own), channel_id=1, source_target_pairs={{0,1},{1,0},{2,3},{3,2},{4,5},{5,4},{6,7},{7,6},{8,9},{9,8},{10,11... | collective-permute-start | bytes 491528 | tf_op jit(solution)/shard_map/ppermute | solution.py:349

commit v6 on v2

--- a/solution.py
+++ b/solution.py
@@ -16,11 +16,15 @@
 SCORE_SCALE = HEAD_DIM ** -0.5
 
 UNIT = 8
-CHUNK_UNITS = 4
+CHUNK_UNITS = 2
 ROWS = UNIT * HEADS
 PACKET = 2 * ROWS + 8
+SCATTER_GROUPS = ((0, 2), (2, 5))
+WHOLE_GROUPS = ((10, 13), (13, 16))
 PIECES = 2
-AHEAD = 3
+FIRST_LAG = 2
+SECOND_LAG = 8
+SCATTERED = 10
 MESH = pl.DeviceIdType.MESH
 F32 = jnp.float32
 BF16 = jnp.bfloat16
@@ -31,8 +35,8 @@
     k_vm, v_vm = rest[:PIECES], rest[PIECES:2 * PIECES]
     (x_new, k_new, v_new, sp_new,
                   pos, freq, x_in, ns, wk, wv, wq, sp, wo, bo,
-                  pos_b, x_f, q_s, pk, rc1, cm, rc2, o_s, ag,
-                  in_sem, k_sem, v_sem, s1, r1, s2, r2, sa, ra, sb, rb, sc, rc) = rest[2 * PIECES:]
+                  pos_b, x_f, q_s, pk, rc1, ch, o_s, ag, agd,
+                  in_sem, k_sem, v_sem, s1, r1, s2, r2, sa, ra, sb, rb, sc, rc, sd, rd) = rest[2 * PIECES:]
     me = lax.axis_index('kv')
     x_side, core = me // 2, me % 2
     over = {'kv': 2 * (1 - x_side) + core}
@@ -41,7 +45,6 @@
     batch, slots = sp.shape
     chunk = UNIT * CHUNK_UNITS
     chunks = batch // chunk
-    half = chunks // 2
 
     barrier = pltpu.get_barrier_semaphore()
     pl.semaphore_signal(barrier, inc=1, device_id=over, device_id_type=MESH)
@@ -64,7 +67,7 @@
 
     for small in smalls[:8]:
         small.start()
-    read_ahead(0, AHEAD)
+    read_ahead(0, 2)
 
     smalls[0].wait()
     smalls[1].wait()
@@ -80,21 +83,23 @@
     def rotate(first):
         return first * cos_t + pltpu.roll(first, ROPE_DIM // 2, 1) * sin_t
 
-    read_ahead(AHEAD, AHEAD + 1)
+    read_ahead(2, 4)
     smalls[2].wait()
     smalls[3].wait()
     x32 = x_in[...].astype(F32)
     x_f[...] = x32
     mean_sq = jnp.mean(x32 * x32, axis=-1, keepdims=True)
     normed = (x32 * lax.rsqrt(mean_sq + EPS) * (1.0 + ns[...].astype(F32)[None, :])).astype(BF16)
+    read_ahead(4, 6)
     smalls[4].wait()
     smalls[5].wait()
+    read_ahead(6, 8)
     k_row = jnp.dot(normed, wk[...], preferred_element_type=F32)
     k_new[:, :128] = rotate(k_row[:, :128]).astype(BF16).astype(F32)
     k_new[:, 128:] = k_row[:, 128:].astype(BF16).astype(F32)
     v_new[...] = jnp.dot(normed, wv[...], preferred_element_type=F32).astype(BF16).astype(F32)
     smalls[6].wait()
-    read_ahead(AHEAD + 1, chunks)
+    read_ahead(8, chunks)
     for small in smalls[8:]:
         small.start()
     for h in range(HEADS):
@@ -167,47 +172,69 @@
         return tile, parts, totals
 
     def first_copy(j):
-        return pltpu.make_async_remote_copy(pk.at[j, pl.ds(2 * (1 - core), 2)], rc1.at[j], s1.at[j], r1.at[j], device_id=beside, device_id_type=MESH)
+        return pltpu.make_async_remote_copy(pk.at[j, 1 - core], rc1.at[j], s1.at[j], r1.at[j], device_id=beside, device_id_type=MESH)
 
     def second_copy(j):
-        return pltpu.make_async_remote_copy(cm.at[j, 1 - x_side], rc2.at[j], s2.at[j], r2.at[j], device_id=over, device_id_type=MESH)
+        rows = ch.at[j, x_side]
+        return pltpu.make_async_remote_copy(rows, rows, s2.at[j], r2.at[j], device_id=over, device_id_type=MESH)
 
     def first_merge(j):
         first_copy(j).wait_recv()
-        for i in range(2):
-            tile, parts, totals = merge(pk[j, 2 * core + i], rc1[j, i])
+        tile, parts, totals = merge(pk[j, core], rc1[j])
+        for h in range(HEADS):
+            ch[j, x_side, h * UNIT:(h + 1) * UNIT, :] = parts[h][0]
+            ch[j, x_side, ROWS + h * UNIT:ROWS + (h + 1) * UNIT, :] = parts[h][1]
+            tile = jnp.where(lane == HEADS + h, totals[h], tile)
+        ch[j, x_side, 2 * ROWS:, :] = tile
+
+        @pl.when((j >= SCATTERED) | (j % 2 != x_side))
+        def _():
+            second_copy(j).start()
+
+    def final_rows(j):
+        return jnp.where(j < SCATTERED, j // 2, j - SCATTERED // 2) * UNIT
+
+    def second_merge(j):
+        @pl.when((j >= SCATTERED) | (j % 2 == x_side))
+        def _():
+            second_copy(j).wait_recv()
+            _, parts, totals = merge(ch[j, 0], ch[j, 1])
+            rows = pl.ds(pl.multiple_of((j // 2 if j < SCATTERED else j - SCATTERED // 2) * UNIT if isinstance(j, int) else final_rows(j), UNIT), UNIT)
             for h in range(HEADS):
-                cm[j, i, h * UNIT:(h + 1) * UNIT, :] = parts[h][0]
-                cm[j, i, ROWS + h * UNIT:ROWS + (h + 1) * UNIT, :] = parts[h][1]
-                tile = jnp.where(lane == HEADS + h, totals[h], tile)
-            cm[j, i, 2 * ROWS:, :] = tile
-        second_copy(j).start()
-
-    def second_merge(j):
-        second_copy(j).wait_recv()
-        _, parts, totals = merge(cm[j, x_side], rc2[j])
-        rows = pl.ds(j * UNIT, UNIT)
-        for h in range(HEADS):
-            inverse = 1.0 / totals[h]
-            o_s[rows, h * HEAD_DIM:h * HEAD_DIM + 128] = parts[h][0] * inverse
-            o_s[rows, h * HEAD_DIM + 128:(h + 1) * HEAD_DIM] = parts[h][1] * inverse
-
-    own_unit = 2 * core + x_side
+                inverse = 1.0 / totals[h]
+                o_s[rows, h * HEAD_DIM:h * HEAD_DIM + 128] = parts[h][0] * inverse
+                o_s[rows, h * HEAD_DIM + 128:(h + 1) * HEAD_DIM] = parts[h][1] * inverse
+
+    def project(first, residual):
+        rows = pl.ds(first, residual.shape[0])
+        return residual + jnp.dot(o_s[rows, :].astype(BF16), wo[...], preferred_element_type=F32) + bo[...].astype(F32)[None, :]
 
     def gather_copy(g, owner, target, send, recv):
-        rows = ag.at[owner, pl.ds(g * half * UNIT, half * UNIT)]
+        first, last = SCATTER_GROUPS[g]
+        rows = ag.at[owner, pl.ds(first * UNIT, (last - first) * UNIT)]
         return pltpu.make_async_remote_copy(rows, rows, send.at[g], recv.at[g], device_id=target, device_id_type=MESH)
 
-    def project(g):
-        o_b = o_s[pl.ds(g * half * UNIT, half * UNIT), :].astype(BF16)
-        rows = jnp.concatenate([x_f[pl.ds((g * half + i) * chunk + own_unit * UNIT, UNIT), :] for i in range(half)], axis=0)
-        ag[me, pl.ds(g * half * UNIT, half * UNIT), :] = rows + jnp.dot(o_b, wo[...], preferred_element_type=F32) + bo[...].astype(F32)[None, :]
+    def project_scattered(g):
+        first, last = SCATTER_GROUPS[g]
+        residual = jnp.concatenate([x_f[pl.ds((2 * i + x_side) * chunk + core * UNIT, UNIT), :] for i in range(first, last)], axis=0)
+        ag[me, first * UNIT:last * UNIT, :] = project(first * UNIT, residual)
         gather_copy(g, me, over, sa, ra).start()
         gather_copy(g, me, beside, sb, rb).start()
 
     def forward(g):
         gather_copy(g, me, over, sa, ra).wait_recv()
         gather_copy(g, over_i, beside, sc, rc).start()
+
+    def beside_copy(g):
+        first, last = WHOLE_GROUPS[g]
+        rows = agd.at[core, pl.ds((first - SCATTERED) * UNIT, (last - first) * UNIT)]
+        return pltpu.make_async_remote_copy(rows, rows, sd.at[g], rd.at[g], device_id=beside, device_id_type=MESH)
+
+    def project_whole(g):
+        first, last = WHOLE_GROUPS[g]
+        residual = jnp.concatenate([x_f[pl.ds(j * chunk + core * UNIT, UNIT), :] for j in range(first, last)], axis=0)
+        agd[core, (first - SCATTERED) * UNIT:(last - SCATTERED) * UNIT, :] = project((first - SCATTERED // 2) * UNIT, residual)
+        beside_copy(g).start()
 
     def step(piece, j, carry):
         for copy in cache_copy(j, piece):
@@ -215,49 +242,68 @@
         attend(j, piece)
         first_copy(j).start()
 
-        @pl.when(j >= 1)
-        def _():
-            first_merge(j - 1)
-
-        @pl.when(j >= 3)
-        def _():
-            second_merge(j - 3)
-
-        @pl.when(j == half + 2)
+        @pl.when(j >= FIRST_LAG)
+        def _():
+            first_merge(j - FIRST_LAG)
+
+        @pl.when(j >= SECOND_LAG)
+        def _():
+            second_merge(j - SECOND_LAG)
+
+        @pl.when(j == 2 * SCATTER_GROUPS[0][1] - 1 + SECOND_LAG)
         def _():
             smalls[8].wait()
             smalls[9].wait()
-            project(0)
+            project_scattered(0)
 
         return carry
 
     for piece in range(PIECES):
         lax.fori_loop(piece * span, (piece + 1) * span, functools.partial(step, piece), 0)
-    second_merge(chunks - 3)
+    for j in range(chunks - FIRST_LAG, chunks):
+        first_merge(j)
+    done = chunks - SECOND_LAG
+    for g in range(1, len(SCATTER_GROUPS)):
+        for j in range(done, 2 * SCATTER_GROUPS[g][1]):
+            second_merge(j)
+        done = max(done, 2 * SCATTER_GROUPS[g][1])
+        project_scattered(g)
     forward(0)
-    first_merge(chunks - 1)
-    second_merge(chunks - 2)
-    second_merge(chunks - 1)
-    project(1)
-    forward(1)
-    for g in range(2):
+    for g in range(len(WHOLE_GROUPS)):
+        for j in range(done, WHOLE_GROUPS[g][1]):
+            second_merge(j)
+        done = WHOLE_GROUPS[g][1]
+        project_whole(g)
+        if g == 0:
+            for early in range(1, len(SCATTER_GROUPS)):
+                forward(early)
+    for g in range(len(SCATTER_GROUPS)):
         gather_copy(g, me, beside, sb, rb).wait_recv()
         gather_copy(g, me, beside, sc, rc).wait_recv()
-    for c in range(2):
-        for j in range(chunks):
-            rows = [ag[2 * s + c, j * UNIT:(j + 1) * UNIT, :] for s in range(2)]
-            x_new[j * chunk + 2 * UNIT * c:j * chunk + 2 * UNIT * (c + 1), :] = jnp.concatenate(rows, axis=0).astype(BF16)
+    for j in range(SCATTERED):
+        rows = [ag[2 * (j % 2) + c, j // 2 * UNIT:(j // 2 + 1) * UNIT, :] for c in range(2)]
+        x_new[j * chunk:(j + 1) * chunk, :] = jnp.concatenate(rows, axis=0).astype(BF16)
+    for g in range(len(WHOLE_GROUPS)):
+        beside_copy(g).wait_recv()
+        for j in range(*WHOLE_GROUPS[g]):
+            rows = [agd[c, (j - SCATTERED) * UNIT:(j - SCATTERED + 1) * UNIT, :] for c in range(2)]
+            x_new[j * chunk:(j + 1) * chunk, :] = jnp.concatenate(rows, axis=0).astype(BF16)
 
     def drain(j, carry):
         first_copy(j).wait_send()
-        second_copy(j).wait_send()
+
+        @pl.when((j >= SCATTERED) | (j % 2 != x_side))
+        def _():
+            second_copy(j).wait_send()
         return carry
 
     lax.fori_loop(0, chunks, drain, 0)
-    for g in range(2):
+    for g in range(len(SCATTER_GROUPS)):
         gather_copy(g, me, over, sa, ra).wait_send()
         gather_copy(g, me, beside, sb, rb).wait_send()
         gather_copy(g, over_i, beside, sc, rc).wait_send()
+    for g in range(len(WHOLE_GROUPS)):
+        beside_copy(g).wait_send()
 
 
 def write_kernel(window, pos, k_new, v_new, x_new, sp_new, *rest):
@@ -345,10 +391,10 @@
                 pltpu.VMEM((model, HEAD_DIM), BF16), pltpu.VMEM((model, HEAD_DIM), BF16), pltpu.VMEM((model, width), BF16),
                 pltpu.VMEM((batch, slots), jnp.int32), pltpu.VMEM((width, model), BF16), pltpu.VMEM((model,), BF16),
                 pltpu.VMEM((batch, 128), F32), pltpu.VMEM((batch, model), F32), pltpu.VMEM((batch // UNIT, HEADS, UNIT, HEAD_DIM), F32),
-                pltpu.VMEM((chunks, CHUNK_UNITS, PACKET, 128), F32), pltpu.VMEM((chunks, 2, PACKET, 128), F32),
-                pltpu.VMEM((chunks, 2, PACKET, 128), F32), pltpu.VMEM((chunks, PACKET, 128), F32),
-                pltpu.VMEM((chunks * UNIT, width), F32), pltpu.VMEM((kv_size, chunks * UNIT, model), F32),
-                dma((10,)), dma((chunks,)), dma((chunks,)), *per_chunk, *([dma((2,))] * 6)],
+                pltpu.VMEM((chunks, CHUNK_UNITS, PACKET, 128), F32), pltpu.VMEM((chunks, PACKET, 128), F32), pltpu.VMEM((chunks, 2, PACKET, 128), F32),
+                pltpu.VMEM(((chunks - SCATTERED // 2) * UNIT, width), F32), pltpu.VMEM((kv_size, SCATTERED // 2 * UNIT, model), F32),
+                pltpu.VMEM((2, (chunks - SCATTERED) * UNIT, model), F32),
+                dma((10,)), dma((chunks,)), dma((chunks,)), *per_chunk, *([dma((len(SCATTER_GROUPS),))] * 6), *([dma((len(WHOLE_GROUPS),))] * 2)],
             compiler_params=pltpu.CompilerParams(vmem_limit_bytes=16 << 20, collective_id=0, has_side_effects=True),
             name='attend',
         )(*[pltpu.with_memory_space_constraint(a, pltpu.HBM) for a in (

time: 41.6 us -> 40.6 us (0.976)
  Pallas kernels: 40.9 us -> 39.8 us
    pallas_call x1, Pallas kernels: 29.1 us -> 28 us  [local_step(): pl.pallas_call(functools.partial(attend_kernel, window), out_shape=(*[plt...]
where the time goes in v6:
time: 40.6 us; the launch traced here: 40.5 us
  Pallas kernels  39.8 us (98%)
  between operations  0.66 us (2%)
    pallas_call x1, Pallas kernels, local_step(): pl.pallas_call(functools.partial(attend_kernel, window), out_shape=(*[plt...  28 us
    pallas_call x1, Pallas kernels, local_step(): pl.pallas_call(functools.partial(write_kernel, window), out_shape=(jax.Sh...  11.8 us

profile of v6, /device:TPU:0, one launch (start us, length us, event | category | flops | bytes accessed | tf_op | source)
XLA Modules:
  0.0 40.5 jit_solution(4261430185428774919)
XLA Ops:
  0.6 0.0 copy-start
  0.6 28.0 %attend.1 = (bf16[128,128,256]{2,1,0:T(8,128)(2,1)S(1)}, bf16[128,128,256]{2,1,0:T(8,128)(2,1)S(1)}, bf16[128,128,256]{2,1,0:T(8,128)(2,1)S(1)}, bf16[128,128,25...) custom-call(s32[2,128]{1,0:T(2,128)} %bitcast.1, ...), custom_call_target="tpu_custom_call" | custom-call | tf_op jit(solution)/shard_map/attend/pallas_call | solution.py:383
  28.7 0.0 copy-done
  28.7 11.8 %write.1 = (bf16[256,640]{1,0:T(8,128)(2,1)}, bf16[256,128,256]{2,1,0:T(8,128)(2,1)}, bf16[256,128,256]{2,1,0:T(8,128)(2,1)}, s32[256,128]{1,0:T(8,128)}) custom-call(s32[256]{0:T(256)S(1)} %copy-done, f32[256,256]{1,0:T(8,128)S(1)} %get-tuple-element.12.k_new, f32[256,256]{1,0:T(8,128)S(1)} %get-tuple-element.13.v_new, ...), custom_call_target="tpu_custom_call" | custom-call | tf_op jit(solution)/shard_map/write/pallas_call | solution.py:403
Async XLA Ops:
  0.6 28.1 %copy-start = (s32[256]{0:T(256)S(1)}, s32[256]{0:T(256)}, u32[]{:S(2)}) copy-start(s32[256]{0:T(256)} %pos.1) | copy-start | bytes 3076

commit v7 on v6

--- a/solution.py
+++ b/solution.py
@@ -22,6 +22,7 @@
 SCATTER_GROUPS = ((0, 2), (2, 5))
 WHOLE_GROUPS = ((10, 13), (13, 16))
 PIECES = 2
+AHEAD = 4
 FIRST_LAG = 2
 SECOND_LAG = 8
 SCATTERED = 10
@@ -74,6 +75,7 @@
     for r in range(batch // 128):
         row = pos[r:r + 1, :].astype(F32)
         pos_b[pl.ds(128 * r, 128), :] = jnp.transpose(jnp.broadcast_to(row, (128, 128)))
+    read_ahead(2, AHEAD)
     angles = pos_b[...] * freq[...]
     low = lax.broadcasted_iota(jnp.int32, (batch, 128), 1) < ROPE_DIM // 2
     cos_t = jnp.cos(angles)
@@ -83,23 +85,19 @@
     def rotate(first):
         return first * cos_t + pltpu.roll(first, ROPE_DIM // 2, 1) * sin_t
 
-    read_ahead(2, 4)
     smalls[2].wait()
     smalls[3].wait()
     x32 = x_in[...].astype(F32)
     x_f[...] = x32
     mean_sq = jnp.mean(x32 * x32, axis=-1, keepdims=True)
     normed = (x32 * lax.rsqrt(mean_sq + EPS) * (1.0 + ns[...].astype(F32)[None, :])).astype(BF16)
-    read_ahead(4, 6)
     smalls[4].wait()
     smalls[5].wait()
-    read_ahead(6, 8)
     k_row = jnp.dot(normed, wk[...], preferred_element_type=F32)
     k_new[:, :128] = rotate(k_row[:, :128]).astype(BF16).astype(F32)
     k_new[:, 128:] = k_row[:, 128:].astype(BF16).astype(F32)
     v_new[...] = jnp.dot(normed, wv[...], preferred_element_type=F32).astype(BF16).astype(F32)
     smalls[6].wait()
-    read_ahead(8, chunks)
     for small in smalls[8:]:
         small.start()
     for h in range(HEADS):
@@ -255,6 +253,12 @@
             smalls[8].wait()
             smalls[9].wait()
             project_scattered(0)
+
+        for ahead in range(PIECES):
+            @pl.when((j + AHEAD < chunks) & ((j + AHEAD) // span == ahead))
+            def _():
+                for copy in cache_copy(j + AHEAD, ahead):
+                    copy.start()
 
         return carry
 

time: 40.6 us -> 40.6 us (level)
  no operation moved by 1% of the time
where the time goes in v7:
time: 40.6 us; the launch traced here: 40.5 us
  Pallas kernels  39.9 us (98%)
  between operations  0.66 us (2%)
    pallas_call x1, Pallas kernels, local_step(): pl.pallas_call(functools.partial(attend_kernel, window), out_shape=(*[plt...  28.1 us
    pallas_call x1, Pallas kernels, local_step(): pl.pallas_call(functools.partial(write_kernel, window), out_shape=(jax.Sh...  11.8 us

profile of v7, /device:TPU:0, one launch (start us, length us, event | category | flops | bytes accessed | tf_op | source)
XLA Modules:
  0.0 40.5 jit_solution(3898407213020149447)
XLA Ops:
  0.6 0.0 copy-start
  0.6 28.1 %attend.1 = (bf16[128,128,256]{2,1,0:T(8,128)(2,1)S(1)}, bf16[128,128,256]{2,1,0:T(8,128)(2,1)S(1)}, bf16[128,128,256]{2,1,0:T(8,128)(2,1)S(1)}, bf16[128,128,25...) custom-call(s32[2,128]{1,0:T(2,128)} %bitcast.1, ...), custom_call_target="tpu_custom_call" | custom-call | tf_op jit(solution)/shard_map/attend/pallas_call | solution.py:387
  28.7 0.0 copy-done
  28.7 11.8 %write.1 = (bf16[256,640]{1,0:T(8,128)(2,1)}, bf16[256,128,256]{2,1,0:T(8,128)(2,1)}, bf16[256,128,256]{2,1,0:T(8,128)(2,1)}, s32[256,128]{1,0:T(8,128)}) custom-call(s32[256]{0:T(256)S(1)} %copy-done, f32[256,256]{1,0:T(8,128)S(1)} %get-tuple-element.12.k_new, f32[256,256]{1,0:T(8,128)S(1)} %get-tuple-element.13.v_new, ...), custom_call_target="tpu_custom_call" | custom-call | tf_op jit(solution)/shard_map/write/pallas_call | solution.py:407
Async XLA Ops:
  0.6 28.1 %copy-start = (s32[256]{0:T(256)S(1)}, s32[256]{0:T(256)}, u32[]{:S(2)}) copy-start(s32[256]{0:T(256)} %pos.1) | copy-start | bytes 3076

commit v8 on v7

--- a/solution.py
+++ b/solution.py
@@ -19,13 +19,12 @@
 CHUNK_UNITS = 2
 ROWS = UNIT * HEADS
 PACKET = 2 * ROWS + 8
-SCATTER_GROUPS = ((0, 2), (2, 5))
-WHOLE_GROUPS = ((10, 13), (13, 16))
+WHOLE_GROUPS = ((0, 4), (10, 13), (13, 16))
 PIECES = 2
 AHEAD = 4
-FIRST_LAG = 2
-SECOND_LAG = 8
-SCATTERED = 10
+FIRST_LAG = 3
+SECOND_LAG = 12
+SCATTER_FIRST, SCATTER_LAST = 4, 10
 MESH = pl.DeviceIdType.MESH
 F32 = jnp.float32
 BF16 = jnp.bfloat16
@@ -37,7 +36,7 @@
     (x_new, k_new, v_new, sp_new,
                   pos, freq, x_in, ns, wk, wv, wq, sp, wo, bo,
                   pos_b, x_f, q_s, pk, rc1, ch, o_s, ag, agd,
-                  in_sem, k_sem, v_sem, s1, r1, s2, r2, sa, ra, sb, rb, sc, rc, sd, rd) = rest[2 * PIECES:]
+                  in_sem, k_sem, v_sem, s1, r1, s2, r2, sa, ra, sd, rd) = rest[2 * PIECES:]
     me = lax.axis_index('kv')
     x_side, core = me // 2, me % 2
     over = {'kv': 2 * (1 - x_side) + core}
@@ -68,14 +67,14 @@
 
     for small in smalls[:8]:
         small.start()
-    read_ahead(0, 2)
+    read_ahead(0, 1)
 
     smalls[0].wait()
     smalls[1].wait()
     for r in range(batch // 128):
         row = pos[r:r + 1, :].astype(F32)
         pos_b[pl.ds(128 * r, 128), :] = jnp.transpose(jnp.broadcast_to(row, (128, 128)))
-    read_ahead(2, AHEAD)
+    read_ahead(1, 2)
     angles = pos_b[...] * freq[...]
     low = lax.broadcasted_iota(jnp.int32, (batch, 128), 1) < ROPE_DIM // 2
     cos_t = jnp.cos(angles)
@@ -87,6 +86,7 @@
 
     smalls[2].wait()
     smalls[3].wait()
+    read_ahead(2, AHEAD)
     x32 = x_in[...].astype(F32)
     x_f[...] = x32
     mean_sq = jnp.mean(x32 * x32, axis=-1, keepdims=True)
@@ -185,19 +185,26 @@
             tile = jnp.where(lane == HEADS + h, totals[h], tile)
         ch[j, x_side, 2 * ROWS:, :] = tile
 
-        @pl.when((j >= SCATTERED) | (j % 2 != x_side))
+        @pl.when((j < SCATTER_FIRST) | (j >= SCATTER_LAST) | (j % 2 != x_side))
         def _():
             second_copy(j).start()
 
-    def final_rows(j):
-        return jnp.where(j < SCATTERED, j // 2, j - SCATTERED // 2) * UNIT
+    scattered = (SCATTER_LAST - SCATTER_FIRST) // 2
+
+    def final_block(j):
+        if isinstance(j, int):
+            return j if j < SCATTER_FIRST else SCATTER_FIRST + (j - SCATTER_FIRST) // 2 if j < SCATTER_LAST else j - scattered
+        return jnp.where(j < SCATTER_FIRST, j, jnp.where(j < SCATTER_LAST, SCATTER_FIRST + (j - SCATTER_FIRST) // 2, j - scattered))
+
+    def whole_block(j):
+        return j if j < SCATTER_FIRST else j - 2 * scattered
 
     def second_merge(j):
-        @pl.when((j >= SCATTERED) | (j % 2 == x_side))
+        @pl.when((j < SCATTER_FIRST) | (j >= SCATTER_LAST) | (j % 2 == x_side))
         def _():
             second_copy(j).wait_recv()
             _, parts, totals = merge(ch[j, 0], ch[j, 1])
-            rows = pl.ds(pl.multiple_of((j // 2 if j < SCATTERED else j - SCATTERED // 2) * UNIT if isinstance(j, int) else final_rows(j), UNIT), UNIT)
+            rows = pl.ds(final_block(j) * UNIT, UNIT)
             for h in range(HEADS):
                 inverse = 1.0 / totals[h]
                 o_s[rows, h * HEAD_DIM:h * HEAD_DIM + 128] = parts[h][0] * inverse
@@ -207,32 +214,34 @@
         rows = pl.ds(first, residual.shape[0])
         return residual + jnp.dot(o_s[rows, :].astype(BF16), wo[...], preferred_element_type=F32) + bo[...].astype(F32)[None, :]
 
-    def gather_copy(g, owner, target, send, recv):
-        first, last = SCATTER_GROUPS[g]
-        rows = ag.at[owner, pl.ds(first * UNIT, (last - first) * UNIT)]
-        return pltpu.make_async_remote_copy(rows, rows, send.at[g], recv.at[g], device_id=target, device_id_type=MESH)
-
-    def project_scattered(g):
-        first, last = SCATTER_GROUPS[g]
-        residual = jnp.concatenate([x_f[pl.ds((2 * i + x_side) * chunk + core * UNIT, UNIT), :] for i in range(first, last)], axis=0)
-        ag[me, first * UNIT:last * UNIT, :] = project(first * UNIT, residual)
-        gather_copy(g, me, over, sa, ra).start()
-        gather_copy(g, me, beside, sb, rb).start()
-
-    def forward(g):
-        gather_copy(g, me, over, sa, ra).wait_recv()
-        gather_copy(g, over_i, beside, sc, rc).start()
+    def gather_copy(owner, target, n):
+        rows = ag.at[owner]
+        return pltpu.make_async_remote_copy(rows, rows, sa.at[n], ra.at[n], device_id=target, device_id_type=MESH)
+
+    gather_over, gather_beside, gather_on = gather_copy(me, over, 0), gather_copy(me, beside, 1), gather_copy(over_i, beside, 2)
+
+    def project_scattered():
+        residual = jnp.concatenate([x_f[pl.ds((SCATTER_FIRST + 2 * i + x_side) * chunk + core * UNIT, UNIT), :] for i in range(scattered)], axis=0)
+        ag[me] = project(SCATTER_FIRST * UNIT, residual)
+        gather_over.start()
+        gather_beside.start()
 
     def beside_copy(g):
         first, last = WHOLE_GROUPS[g]
-        rows = agd.at[core, pl.ds((first - SCATTERED) * UNIT, (last - first) * UNIT)]
+        rows = agd.at[core, pl.ds(whole_block(first) * UNIT, (last - first) * UNIT)]
         return pltpu.make_async_remote_copy(rows, rows, sd.at[g], rd.at[g], device_id=beside, device_id_type=MESH)
 
     def project_whole(g):
         first, last = WHOLE_GROUPS[g]
         residual = jnp.concatenate([x_f[pl.ds(j * chunk + core * UNIT, UNIT), :] for j in range(first, last)], axis=0)
-        agd[core, (first - SCATTERED) * UNIT:(last - SCATTERED) * UNIT, :] = project((first - SCATTERED // 2) * UNIT, residual)
+        agd[core, whole_block(first) * UNIT:whole_block(last - 1) * UNIT + UNIT, :] = project(final_block(first) * UNIT, residual)
         beside_copy(g).start()
+
+    def collect_whole(g):
+        beside_copy(g).wait_recv()
+        for j in range(*WHOLE_GROUPS[g]):
+            rows = [agd[c, whole_block(j) * UNIT:(whole_block(j) + 1) * UNIT, :] for c in range(2)]
+            x_new[j * chunk:(j + 1) * chunk, :] = jnp.concatenate(rows, axis=0).astype(BF16)
 
     def step(piece, j, carry):
         for copy in cache_copy(j, piece):
@@ -248,12 +257,6 @@
         def _():
             second_merge(j - SECOND_LAG)
 
-        @pl.when(j == 2 * SCATTER_GROUPS[0][1] - 1 + SECOND_LAG)
-        def _():
-            smalls[8].wait()
-            smalls[9].wait()
-            project_scattered(0)
-
         for ahead in range(PIECES):
             @pl.when((j + AHEAD < chunks) & ((j + AHEAD) // span == ahead))
             def _():
@@ -266,46 +269,43 @@
         lax.fori_loop(piece * span, (piece + 1) * span, functools.partial(step, piece), 0)
     for j in range(chunks - FIRST_LAG, chunks):
         first_merge(j)
-    done = chunks - SECOND_LAG
-    for g in range(1, len(SCATTER_GROUPS)):
-        for j in range(done, 2 * SCATTER_GROUPS[g][1]):
+    for small in smalls[8:]:
+        small.wait()
+    for j in range(chunks - SECOND_LAG, SCATTER_LAST):
+        second_merge(j)
+    project_scattered()
+    project_whole(0)
+    for j in range(*WHOLE_GROUPS[1]):
+        second_merge(j)
+    project_whole(1)
+    collect_whole(0)
+    gather_over.wait_recv()
+    gather_on.start()
+    for g in range(2, len(WHOLE_GROUPS)):
+        for j in range(*WHOLE_GROUPS[g]):
             second_merge(j)
-        done = max(done, 2 * SCATTER_GROUPS[g][1])
-        project_scattered(g)
-    forward(0)
-    for g in range(len(WHOLE_GROUPS)):
-        for j in range(done, WHOLE_GROUPS[g][1]):
-            second_merge(j)
-        done = WHOLE_GROUPS[g][1]
         project_whole(g)
-        if g == 0:
-            for early in range(1, len(SCATTER_GROUPS)):
-                forward(early)
-    for g in range(len(SCATTER_GROUPS)):
-        gather_copy(g, me, beside, sb, rb).wait_recv()
-        gather_copy(g, me, beside, sc, rc).wait_recv()
-    for j in range(SCATTERED):
-        rows = [ag[2 * (j % 2) + c, j // 2 * UNIT:(j // 2 + 1) * UNIT, :] for c in range(2)]
+    collect_whole(1)
+    gather_beside.wait_recv()
+    gather_on.wait_recv()
+    for j in range(SCATTER_FIRST, SCATTER_LAST):
+        i = (j - SCATTER_FIRST) // 2
+        rows = [ag[2 * (j % 2) + c, i * UNIT:(i + 1) * UNIT, :] for c in range(2)]
         x_new[j * chunk:(j + 1) * chunk, :] = jnp.concatenate(rows, axis=0).astype(BF16)
-    for g in range(len(WHOLE_GROUPS)):
-        beside_copy(g).wait_recv()
-        for j in range(*WHOLE_GROUPS[g]):
-            rows = [agd[c, (j - SCATTERED) * UNIT:(j - SCATTERED + 1) * UNIT, :] for c in range(2)]
-            x_new[j * chunk:(j + 1) * chunk, :] = jnp.concatenate(rows, axis=0).astype(BF16)
+    for g in range(2, len(WHOLE_GROUPS)):
+        collect_whole(g)
 
     def drain(j, carry):
         first_copy(j).wait_send()
 
-        @pl.when((j >= SCATTERED) | (j % 2 != x_side))
+        @pl.when((j < SCATTER_FIRST) | (j >= SCATTER_LAST) | (j % 2 != x_side))
         def _():
             second_copy(j).wait_send()
         return carry
 
     lax.fori_loop(0, chunks, drain, 0)
-    for g in range(len(SCATTER_GROUPS)):
-        gather_copy(g, me, over, sa, ra).wait_send()
-        gather_copy(g, me, beside, sb, rb).wait_send()
-        gather_copy(g, over_i, beside, sc, rc).wait_send()
+    for gather in (gather_over, gather_beside, gather_on):
+        gather.wait_send()
     for g in range(len(WHOLE_GROUPS)):
         beside_copy(g).wait_send()
 
@@ -379,6 +379,7 @@
         window = slots * kv_size
         width = w_q.shape[1]
         chunks = batch // (UNIT * CHUNK_UNITS)
+        scattered = (SCATTER_LAST - SCATTER_FIRST) // 2
         hbm = pl.BlockSpec(memory_space=pltpu.HBM)
         vmem = pl.BlockSpec(memory_space=pltpu.VMEM)
         smem = pl.BlockSpec(memory_space=pltpu.SMEM)
@@ -396,9 +397,9 @@
                 pltpu.VMEM((batch, slots), jnp.int32), pltpu.VMEM((width, model), BF16), pltpu.VMEM((model,), BF16),
                 pltpu.VMEM((batch, 128), F32), pltpu.VMEM((batch, model), F32), pltpu.VMEM((batch // UNIT, HEADS, UNIT, HEAD_DIM), F32),
                 pltpu.VMEM((chunks, CHUNK_UNITS, PACKET, 128), F32), pltpu.VMEM((chunks, PACKET, 128), F32), pltpu.VMEM((chunks, 2, PACKET, 128), F32),
-                pltpu.VMEM(((chunks - SCATTERED // 2) * UNIT, width), F32), pltpu.VMEM((kv_size, SCATTERED // 2 * UNIT, model), F32),
-                pltpu.VMEM((2, (chunks - SCATTERED) * UNIT, model), F32),
-                dma((10,)), dma((chunks,)), dma((chunks,)), *per_chunk, *([dma((len(SCATTER_GROUPS),))] * 6), *([dma((len(WHOLE_GROUPS),))] * 2)],
+                pltpu.VMEM(((chunks - scattered) * UNIT, width), F32), pltpu.VMEM((kv_size, scattered * UNIT, model), F32),
+                pltpu.VMEM((2, (chunks - 2 * scattered) * UNIT, model), F32),
+                dma((10,)), dma((chunks,)), dma((chunks,)), *per_chunk, dma((3,)), dma((3,)), *([dma((len(WHOLE_GROUPS),))] * 2)],
             compiler_params=pltpu.CompilerParams(vmem_limit_bytes=16 << 20, collective_id=0, has_side_effects=True),
             name='attend',
         )(*[pltpu.with_memory_space_constraint(a, pltpu.HBM) for a in (

time: 40.6 us -> 40.8 us (level)
  no operation moved by 1% of the time
where the time goes in v8:
time: 40.8 us; the launch traced here: 40.7 us
  Pallas kernels  40 us (98%)
  between operations  0.66 us (2%)
    pallas_call x1, Pallas kernels, local_step(): pl.pallas_call(functools.partial(attend_kernel, window), out_shape=(*[plt...  28.2 us
    pallas_call x1, Pallas kernels, local_step(): pl.pallas_call(functools.partial(write_kernel, window), out_shape=(jax.Sh...  11.8 us

profile of v8, /device:TPU:0, one launch (start us, length us, event | category | flops | bytes accessed | tf_op | source)
XLA Modules:
  0.0 40.7 jit_solution(16835587732627592434)
XLA Ops:
  0.6 0.0 copy-start
  0.6 28.2 %attend.1 = (bf16[128,128,256]{2,1,0:T(8,128)(2,1)S(1)}, bf16[128,128,256]{2,1,0:T(8,128)(2,1)S(1)}, bf16[128,128,256]{2,1,0:T(8,128)(2,1)S(1)}, bf16[128,128,25...) custom-call(s32[2,128]{1,0:T(2,128)} %bitcast.1, ...), custom_call_target="tpu_custom_call" | custom-call | tf_op jit(solution)/shard_map/attend/pallas_call | solution.py:388
  28.9 0.0 copy-done
  28.9 11.8 %write.1 = (bf16[256,640]{1,0:T(8,128)(2,1)}, bf16[256,128,256]{2,1,0:T(8,128)(2,1)}, bf16[256,128,256]{2,1,0:T(8,128)(2,1)}, s32[256,128]{1,0:T(8,128)}) custom-call(s32[256]{0:T(256)S(1)} %copy-done, f32[256,256]{1,0:T(8,128)S(1)} %get-tuple-element.12.k_new, f32[256,256]{1,0:T(8,128)S(1)} %get-tuple-element.13.v_new, ...), custom_call_target="tpu_custom_call" | custom-call | tf_op jit(solution)/shard_map/write/pallas_call | solution.py:408
Async XLA Ops:
  0.6 28.3 %copy-start = (s32[256]{0:T(256)S(1)}, s32[256]{0:T(256)}, u32[]{:S(2)}) copy-start(s32[256]{0:T(256)} %pos.1) | copy-start | bytes 3076

commit v9 on v8

--- a/solution.py
+++ b/solution.py
@@ -19,12 +19,13 @@
 CHUNK_UNITS = 2
 ROWS = UNIT * HEADS
 PACKET = 2 * ROWS + 8
-WHOLE_GROUPS = ((0, 4), (10, 13), (13, 16))
+SCATTER_GROUPS = ((2, 6), (6, 12))
+WHOLE_GROUPS = ((0, 2), (12, 14), (14, 16))
 PIECES = 2
-AHEAD = 4
-FIRST_LAG = 3
-SECOND_LAG = 12
-SCATTER_FIRST, SCATTER_LAST = 4, 10
+AHEAD = 6
+FIRST_LAG = 2
+SECOND_LAG = 10
+SCATTER_FIRST, SCATTER_LAST = 2, 12
 MESH = pl.DeviceIdType.MESH
 F32 = jnp.float32
 BF16 = jnp.bfloat16
@@ -145,18 +146,19 @@
         return sums.reshape(ROWS, HEAD_DIM)
 
     def attend(j, piece):
-        units = [j * CHUNK_UNITS + i for i in range(CHUNK_UNITS)]
+        units = [j * CHUNK_UNITS + i for i in range(2 * CHUNK_UNITS)]
         scored = [scores_of(u, piece) for u in units]
         weighed = [weights_of(u, *pair) for u, pair in zip(units, scored)]
         for i, u in enumerate(units):
             top, total, fresh_weight, spread = weighed[i]
             sums = sums_of(u, piece, fresh_weight, spread)
-            pk[j, i, 0:ROWS, :] = sums[:, :128]
-            pk[j, i, ROWS:2 * ROWS, :] = sums[:, 128:]
+            n, i = j + i // CHUNK_UNITS, i % CHUNK_UNITS
+            pk[n, i, 0:ROWS, :] = sums[:, :128]
+            pk[n, i, ROWS:2 * ROWS, :] = sums[:, 128:]
             tile = jnp.zeros((UNIT, 128), F32)
             for h in range(HEADS):
                 tile = jnp.where(lane == h, top[h], jnp.where(lane == HEADS + h, total[h], tile))
-            pk[j, i, 2 * ROWS:, :] = tile
+            pk[n, i, 2 * ROWS:, :] = tile
 
     def merge(a, b):
         ta, tb = a[2 * ROWS:, :], b[2 * ROWS:, :]
@@ -176,18 +178,32 @@
         rows = ch.at[j, x_side]
         return pltpu.make_async_remote_copy(rows, rows, s2.at[j], r2.at[j], device_id=over, device_id_type=MESH)
 
+    def either(condition, yes, no):
+        if isinstance(condition, bool):
+            return yes() if condition else no()
+        pl.when(condition)(yes)
+        pl.when(jnp.logical_not(condition))(no)
+
+    def is_whole(j):
+        return (j < SCATTER_FIRST or j >= SCATTER_LAST) if isinstance(j, int) else (j < SCATTER_FIRST) | (j >= SCATTER_LAST)
+
     def first_merge(j):
-        first_copy(j).wait_recv()
-        tile, parts, totals = merge(pk[j, core], rc1[j])
-        for h in range(HEADS):
-            ch[j, x_side, h * UNIT:(h + 1) * UNIT, :] = parts[h][0]
-            ch[j, x_side, ROWS + h * UNIT:ROWS + (h + 1) * UNIT, :] = parts[h][1]
-            tile = jnp.where(lane == HEADS + h, totals[h], tile)
-        ch[j, x_side, 2 * ROWS:, :] = tile
-
-        @pl.when((j < SCATTER_FIRST) | (j >= SCATTER_LAST) | (j % 2 != x_side))
-        def _():
-            second_copy(j).start()
+        pair = (j, j + 1)
+        for n in pair:
+            first_copy(n).wait_recv()
+        merged = [merge(pk[n, core], rc1[n]) for n in pair]
+        for n, (tile, parts, totals) in zip(pair, merged):
+            for h in range(HEADS):
+                ch[n, x_side, h * UNIT:(h + 1) * UNIT, :] = parts[h][0]
+                ch[n, x_side, ROWS + h * UNIT:ROWS + (h + 1) * UNIT, :] = parts[h][1]
+                tile = jnp.where(lane == HEADS + h, totals[h], tile)
+            ch[n, x_side, 2 * ROWS:, :] = tile
+
+        def both():
+            for n in pair:
+                second_copy(n).start()
+
+        either(is_whole(j), both, lambda: second_copy(j + 1 - x_side).start())
 
     scattered = (SCATTER_LAST - SCATTER_FIRST) // 2
 
@@ -199,32 +215,50 @@
     def whole_block(j):
         return j if j < SCATTER_FIRST else j - 2 * scattered
 
-    def second_merge(j):
-        @pl.when((j < SCATTER_FIRST) | (j >= SCATTER_LAST) | (j % 2 == x_side))
-        def _():
-            second_copy(j).wait_recv()
-            _, parts, totals = merge(ch[j, 0], ch[j, 1])
-            rows = pl.ds(final_block(j) * UNIT, UNIT)
+    def finish(*chunk_ids):
+        for n in chunk_ids:
+            second_copy(n).wait_recv()
+        merged = [merge(ch[n, 0], ch[n, 1]) for n in chunk_ids]
+        for n, (_, parts, totals) in zip(chunk_ids, merged):
+            rows = pl.ds(final_block(n) * UNIT, UNIT)
             for h in range(HEADS):
                 inverse = 1.0 / totals[h]
                 o_s[rows, h * HEAD_DIM:h * HEAD_DIM + 128] = parts[h][0] * inverse
                 o_s[rows, h * HEAD_DIM + 128:(h + 1) * HEAD_DIM] = parts[h][1] * inverse
 
+    def second_merge(j):
+        either(is_whole(j), lambda: finish(j, j + 1), lambda: finish(j + x_side))
+
     def project(first, residual):
         rows = pl.ds(first, residual.shape[0])
         return residual + jnp.dot(o_s[rows, :].astype(BF16), wo[...], preferred_element_type=F32) + bo[...].astype(F32)[None, :]
 
-    def gather_copy(owner, target, n):
-        rows = ag.at[owner]
-        return pltpu.make_async_remote_copy(rows, rows, sa.at[n], ra.at[n], device_id=target, device_id_type=MESH)
-
-    gather_over, gather_beside, gather_on = gather_copy(me, over, 0), gather_copy(me, beside, 1), gather_copy(over_i, beside, 2)
-
-    def project_scattered():
-        residual = jnp.concatenate([x_f[pl.ds((SCATTER_FIRST + 2 * i + x_side) * chunk + core * UNIT, UNIT), :] for i in range(scattered)], axis=0)
-        ag[me] = project(SCATTER_FIRST * UNIT, residual)
-        gather_over.start()
-        gather_beside.start()
+    def gather_copy(g, owner, target, n):
+        first, last = SCATTER_GROUPS[g]
+        rows = ag.at[owner, pl.ds((first - SCATTER_FIRST) // 2 * UNIT, (last - first) // 2 * UNIT)]
+        return pltpu.make_async_remote_copy(rows, rows, sa.at[g, n], ra.at[g, n], device_id=target, device_id_type=MESH)
+
+    gathers = [(gather_copy(g, me, over, 0), gather_copy(g, me, beside, 1), gather_copy(g, over_i, beside, 2)) for g in range(len(SCATTER_GROUPS))]
+
+    def project_scattered(g):
+        first, last = SCATTER_GROUPS[g]
+        residual = jnp.concatenate([x_f[pl.ds((n + x_side) * chunk + core * UNIT, UNIT), :] for n in range(first, last, 2)], axis=0)
+        start = (first - SCATTER_FIRST) // 2 * UNIT
+        ag[me, start:start + residual.shape[0], :] = project(SCATTER_FIRST * UNIT + start, residual)
+        gathers[g][0].start()
+        gathers[g][1].start()
+
+    def forward(g):
+        gathers[g][0].wait_recv()
+        gathers[g][2].start()
+
+    def collect_scattered(g):
+        gathers[g][1].wait_recv()
+        gathers[g][2].wait_recv()
+        for j in range(*SCATTER_GROUPS[g]):
+            i = (j - SCATTER_FIRST) // 2
+            rows = [ag[2 * (j % 2) + c, i * UNIT:(i + 1) * UNIT, :] for c in range(2)]
+            x_new[j * chunk:(j + 1) * chunk, :] = jnp.concatenate(rows, axis=0).astype(BF16)
 
     def beside_copy(g):
         first, last = WHOLE_GROUPS[g]
@@ -243,11 +277,14 @@
             rows = [agd[c, whole_block(j) * UNIT:(whole_block(j) + 1) * UNIT, :] for c in range(2)]
             x_new[j * chunk:(j + 1) * chunk, :] = jnp.concatenate(rows, axis=0).astype(BF16)
 
-    def step(piece, j, carry):
-        for copy in cache_copy(j, piece):
-            copy.wait()
+    def step(piece, block, carry):
+        j = 2 * block
+        for n in range(2):
+            for copy in cache_copy(j + n, piece):
+                copy.wait()
         attend(j, piece)
-        first_copy(j).start()
+        for n in range(2):
+            first_copy(j + n).start()
 
         @pl.when(j >= FIRST_LAG)
         def _():
@@ -260,39 +297,40 @@
         for ahead in range(PIECES):
             @pl.when((j + AHEAD < chunks) & ((j + AHEAD) // span == ahead))
             def _():
-                for copy in cache_copy(j + AHEAD, ahead):
-                    copy.start()
+                for n in range(2):
+                    for copy in cache_copy(j + AHEAD + n, ahead):
+                        copy.start()
 
         return carry
 
     for piece in range(PIECES):
-        lax.fori_loop(piece * span, (piece + 1) * span, functools.partial(step, piece), 0)
-    for j in range(chunks - FIRST_LAG, chunks):
-        first_merge(j)
+        lax.fori_loop(piece * span // 2, (piece + 1) * span // 2, functools.partial(step, piece), 0)
     for small in smalls[8:]:
         small.wait()
-    for j in range(chunks - SECOND_LAG, SCATTER_LAST):
-        second_merge(j)
-    project_scattered()
+    seconds = list(range(chunks - SECOND_LAG, chunks, 2))
+    firsts = list(range(chunks - FIRST_LAG, chunks, 2))
+
+    def second_upto(last):
+        while seconds and seconds[0] < last:
+            second_merge(seconds.pop(0))
+
+    second_upto(SCATTER_GROUPS[0][1])
+    project_scattered(0)
+    for j in firsts:
+        first_merge(j)
     project_whole(0)
-    for j in range(*WHOLE_GROUPS[1]):
-        second_merge(j)
-    project_whole(1)
+    second_upto(SCATTER_GROUPS[1][1])
+    project_scattered(1)
+    forward(0)
     collect_whole(0)
-    gather_over.wait_recv()
-    gather_on.start()
-    for g in range(2, len(WHOLE_GROUPS)):
-        for j in range(*WHOLE_GROUPS[g]):
-            second_merge(j)
+    for g in range(1, len(WHOLE_GROUPS)):
+        second_upto(WHOLE_GROUPS[g][1])
         project_whole(g)
-    collect_whole(1)
-    gather_beside.wait_recv()
-    gather_on.wait_recv()
-    for j in range(SCATTER_FIRST, SCATTER_LAST):
-        i = (j - SCATTER_FIRST) // 2
-        rows = [ag[2 * (j % 2) + c, i * UNIT:(i + 1) * UNIT, :] for c in range(2)]
-        x_new[j * chunk:(j + 1) * chunk, :] = jnp.concatenate(rows, axis=0).astype(BF16)
-    for g in range(2, len(WHOLE_GROUPS)):
+        if g == 1:
+            collect_scattered(0)
+    forward(1)
+    collect_scattered(1)
+    for g in range(1, len(WHOLE_GROUPS)):
         collect_whole(g)
 
     def drain(j, carry):
@@ -304,8 +342,9 @@
         return carry
 
     lax.fori_loop(0, chunks, drain, 0)
-    for gather in (gather_over, gather_beside, gather_on):
-        gather.wait_send()
+    for group in gathers:
+        for gather in group:
+            gather.wait_send()
     for g in range(len(WHOLE_GROUPS)):
         beside_copy(g).wait_send()
 
@@ -399,7 +438,7 @@
                 pltpu.VMEM((chunks, CHUNK_UNITS, PACKET, 128), F32), pltpu.VMEM((chunks, PACKET, 128), F32), pltpu.VMEM((chunks, 2, PACKET, 128), F32),
                 pltpu.VMEM(((chunks - scattered) * UNIT, width), F32), pltpu.VMEM((kv_size, scattered * UNIT, model), F32),
                 pltpu.VMEM((2, (chunks - 2 * scattered) * UNIT, model), F32),
-                dma((10,)), dma((chunks,)), dma((chunks,)), *per_chunk, dma((3,)), dma((3,)), *([dma((len(WHOLE_GROUPS),))] * 2)],
+                dma((10,)), dma((chunks,)), dma((chunks,)), *per_chunk, *([dma((len(SCATTER_GROUPS), 3))] * 2), *([dma((len(WHOLE_GROUPS),))] * 2)],
             compiler_params=pltpu.CompilerParams(vmem_limit_bytes=16 << 20, collective_id=0, has_side_effects=True),
             name='attend',
         )(*[pltpu.with_memory_space_constraint(a, pltpu.HBM) for a in (

time: 40.8 us -> 37.9 us (0.929)
  Pallas kernels: 40 us -> 37.1 us
    pallas_call x1, Pallas kernels: 28.2 us -> 25.3 us  [local_step(): pl.pallas_call(functools.partial(attend_kernel, window), out_shape=(*[plt...]
where the time goes in v9:
time: 37.9 us; the launch traced here: 37.8 us
  Pallas kernels  37.1 us (98%)
  between operations  0.66 us (2%)
    pallas_call x1, Pallas kernels, local_step(): pl.pallas_call(functools.partial(attend_kernel, window), out_shape=(*[plt...  25.3 us
    pallas_call x1, Pallas kernels, local_step(): pl.pallas_call(functools.partial(write_kernel, window), out_shape=(jax.Sh...  11.8 us

profile of v9, /device:TPU:0, one launch (start us, length us, event | category | flops | bytes accessed | tf_op | source)
XLA Modules:
  0.0 37.8 jit_solution(9556199811832518015)
XLA Ops:
  0.6 0.0 copy-start
  0.6 25.3 %attend.1 = (bf16[128,128,256]{2,1,0:T(8,128)(2,1)S(1)}, bf16[128,128,256]{2,1,0:T(8,128)(2,1)S(1)}, bf16[128,128,256]{2,1,0:T(8,128)(2,1)S(1)}, bf16[128,128,25...) custom-call(s32[2,128]{1,0:T(2,128)} %bitcast.1, ...), custom_call_target="tpu_custom_call" | custom-call | tf_op jit(solution)/shard_map/attend/pallas_call | solution.py:427
  26.0 0.0 copy-done
  26.0 11.8 %write.1 = (bf16[256,640]{1,0:T(8,128)(2,1)}, bf16[256,128,256]{2,1,0:T(8,128)(2,1)}, bf16[256,128,256]{2,1,0:T(8,128)(2,1)}, s32[256,128]{1,0:T(8,128)}) custom-call(s32[256]{0:T(256)S(1)} %copy-done, f32[256,256]{1,0:T(8,128)S(1)} %get-tuple-element.12.k_new, f32[256,256]{1,0:T(8,128)S(1)} %get-tuple-element.13.v_new, ...), custom_call_target="tpu_custom_call" | custom-call | tf_op jit(solution)/shard_map/write/pallas_call | solution.py:447
Async XLA Ops:
  0.6 25.3 %copy-start = (s32[256]{0:T(256)S(1)}, s32[256]{0:T(256)}, u32[]{:S(2)}) copy-start(s32[256]{0:T(256)} %pos.1) | copy-start | bytes 3076

commit v10 on v9

--- a/solution.py
+++ b/solution.py
@@ -24,7 +24,6 @@
 PIECES = 2
 AHEAD = 6
 FIRST_LAG = 2
-SECOND_LAG = 10
 SCATTER_FIRST, SCATTER_LAST = 2, 12
 MESH = pl.DeviceIdType.MESH
 F32 = jnp.float32
@@ -36,7 +35,7 @@
     k_vm, v_vm = rest[:PIECES], rest[PIECES:2 * PIECES]
     (x_new, k_new, v_new, sp_new,
                   pos, freq, x_in, ns, wk, wv, wq, sp, wo, bo,
-                  pos_b, x_f, q_s, pk, rc1, ch, o_s, ag, agd,
+                  pos_b, x_f, q_s, sc_s, pk, rc1, ch, o_s, ag, agd,
                   in_sem, k_sem, v_sem, s1, r1, s2, r2, sa, ra, sd, rd) = rest[2 * PIECES:]
     me = lax.axis_index('kv')
     x_side, core = me // 2, me % 2
@@ -116,11 +115,17 @@
         q_b = q_s[u].reshape(ROWS, HEAD_DIM).astype(BF16)
         return q_b, lax.dot_general(q_b, keys, (((1,), (1,)), ((), ())), preferred_element_type=F32)
 
-    def weights_of(u, q_b, all_scores):
+    def score(j, piece):
+        for i in range(2 * CHUNK_UNITS):
+            _, all_scores = scores_of(j * CHUNK_UNITS + i, piece)
+            scores = all_scores[:, :slots]
+            for s in range(1, UNIT):
+                scores = jnp.where(row_seq == s, all_scores[:, s * slots:(s + 1) * slots], scores)
+            sc_s[i] = scores
+
+    def weights_of(u, scores):
         seqs = pl.ds(u * UNIT, UNIT)
-        scores = all_scores[:, :slots]
-        for s in range(1, UNIT):
-            scores = jnp.where(row_seq == s, all_scores[:, s * slots:(s + 1) * slots], scores)
+        q_b = q_s[u].reshape(ROWS, HEAD_DIM).astype(BF16)
         p_now = pos_b[seqs, :].astype(jnp.int32)
         slot = (p_now & (window - 1)) - me * slots
         hit = lane == slot
@@ -145,10 +150,12 @@
         sums = sums + fresh_weight.astype(BF16).astype(F32) * v_new[pl.ds(u * UNIT, UNIT), :][None]
         return sums.reshape(ROWS, HEAD_DIM)
 
-    def attend(j, piece):
+    def attend(j, piece, next_piece):
         units = [j * CHUNK_UNITS + i for i in range(2 * CHUNK_UNITS)]
-        scored = [scores_of(u, piece) for u in units]
-        weighed = [weights_of(u, *pair) for u, pair in zip(units, scored)]
+        scored = [sc_s[i] for i in range(2 * CHUNK_UNITS)]
+        weighed = [weights_of(u, scores) for u, scores in zip(units, scored)]
+        if next_piece is not None:
+            score(j + 2, next_piece)
         for i, u in enumerate(units):
             top, total, fresh_weight, spread = weighed[i]
             sums = sums_of(u, piece, fresh_weight, spread)
@@ -277,22 +284,19 @@
             rows = [agd[c, whole_block(j) * UNIT:(whole_block(j) + 1) * UNIT, :] for c in range(2)]
             x_new[j * chunk:(j + 1) * chunk, :] = jnp.concatenate(rows, axis=0).astype(BF16)
 
-    def step(piece, block, carry):
+    def step(piece, next_piece, block, carry):
         j = 2 * block
         for n in range(2):
-            for copy in cache_copy(j + n, piece):
-                copy.wait()
-        attend(j, piece)
+            if next_piece is not None:
+                cache_copy(j + 2 + n, next_piece)[0].wait()
+            cache_copy(j + n, piece)[1].wait()
+        attend(j, piece, next_piece)
         for n in range(2):
             first_copy(j + n).start()
 
         @pl.when(j >= FIRST_LAG)
         def _():
             first_merge(j - FIRST_LAG)
-
-        @pl.when(j >= SECOND_LAG)
-        def _():
-            second_merge(j - SECOND_LAG)
 
         for ahead in range(PIECES):
             @pl.when((j + AHEAD < chunks) & ((j + AHEAD) // span == ahead))
@@ -303,11 +307,16 @@
 
         return carry
 
+    for n in range(2):
+        cache_copy(n, 0)[0].wait()
+    score(0, 0)
     for piece in range(PIECES):
-        lax.fori_loop(piece * span // 2, (piece + 1) * span // 2, functools.partial(step, piece), 0)
+        last = (piece + 1) * span // 2 - 1
+        lax.fori_loop(piece * span // 2, last, functools.partial(step, piece, piece), 0)
+        lax.fori_loop(last, last + 1, functools.partial(step, piece, piece + 1 if piece + 1 < PIECES else None), 0)
     for small in smalls[8:]:
         small.wait()
-    seconds = list(range(chunks - SECOND_LAG, chunks, 2))
+    seconds = list(range(0, chunks, 2))
     firsts = list(range(chunks - FIRST_LAG, chunks, 2))
 
     def second_upto(last):
@@ -435,6 +444,7 @@
                 pltpu.VMEM((model, HEAD_DIM), BF16), pltpu.VMEM((model, HEAD_DIM), BF16), pltpu.VMEM((model, width), BF16),
                 pltpu.VMEM((batch, slots), jnp.int32), pltpu.VMEM((width, model), BF16), pltpu.VMEM((model,), BF16),
                 pltpu.VMEM((batch, 128), F32), pltpu.VMEM((batch, model), F32), pltpu.VMEM((batch // UNIT, HEADS, UNIT, HEAD_DIM), F32),
+                pltpu.VMEM((2 * CHUNK_UNITS, ROWS, slots), F32),
                 pltpu.VMEM((chunks, CHUNK_UNITS, PACKET, 128), F32), pltpu.VMEM((chunks, PACKET, 128), F32), pltpu.VMEM((chunks, 2, PACKET, 128), F32),
                 pltpu.VMEM(((chunks - scattered) * UNIT, width), F32), pltpu.VMEM((kv_size, scattered * UNIT, model), F32),
                 pltpu.VMEM((2, (chunks - 2 * scattered) * UNIT, model), F32),

time: 37.9 us -> 40.3 us (1.063)
  Pallas kernels: 37.1 us -> 39.5 us
    pallas_call x1, Pallas kernels: 25.3 us -> 27.7 us  [local_step(): pl.pallas_call(functools.partial(attend_kernel, window), out_shape=(*[plt...]
where the time goes in v10:
time: 40.3 us; the launch traced here: 40.1 us
  Pallas kernels  39.5 us (98%)
  between operations  0.66 us (2%)
    pallas_call x1, Pallas kernels, local_step(): pl.pallas_call(functools.partial(attend_kernel, window), out_shape=(*[plt...  27.7 us
    pallas_call x1, Pallas kernels, local_step(): pl.pallas_call(functools.partial(write_kernel, window), out_shape=(jax.Sh...  11.8 us

profile of v10, /device:TPU:0, one launch (start us, length us, event | category | flops | bytes accessed | tf_op | source)
XLA Modules:
  0.0 40.1 jit_solution(8974740634604052333)
XLA Ops:
  0.6 0.0 copy-start
  0.6 27.7 %attend.1 = (bf16[128,128,256]{2,1,0:T(8,128)(2,1)S(1)}, bf16[128,128,256]{2,1,0:T(8,128)(2,1)S(1)}, bf16[128,128,256]{2,1,0:T(8,128)(2,1)S(1)}, bf16[128,128,25...) custom-call(s32[2,128]{1,0:T(2,128)} %bitcast.1, ...), custom_call_target="tpu_custom_call" | custom-call | tf_op jit(solution)/shard_map/attend/pallas_call | solution.py:436
  28.3 0.0 copy-done
  28.3 11.8 %write.1 = (bf16[256,640]{1,0:T(8,128)(2,1)}, bf16[256,128,256]{2,1,0:T(8,128)(2,1)}, bf16[256,128,256]{2,1,0:T(8,128)(2,1)}, s32[256,128]{1,0:T(8,128)}) custom-call(s32[256]{0:T(256)S(1)} %copy-done, f32[256,256]{1,0:T(8,128)S(1)} %get-tuple-element.12.k_new, f32[256,256]{1,0:T(8,128)S(1)} %get-tuple-element.13.v_new, ...), custom_call_target="tpu_custom_call" | custom-call | tf_op jit(solution)/shard_map/write/pallas_call | solution.py:457
Async XLA Ops:
  0.6 27.7 %copy-start = (s32[256]{0:T(256)S(1)}, s32[256]{0:T(256)}, u32[]{:S(2)}) copy-start(s32[256]{0:T(256)} %pos.1) | copy-start | bytes 3076

commit v11 on v9

--- a/solution.py
+++ b/solution.py
@@ -19,13 +19,13 @@
 CHUNK_UNITS = 2
 ROWS = UNIT * HEADS
 PACKET = 2 * ROWS + 8
-SCATTER_GROUPS = ((2, 6), (6, 12))
-WHOLE_GROUPS = ((0, 2), (12, 14), (14, 16))
+SCATTER_GROUPS = ((4, 8), (8, 12))
+WHOLE_GROUPS = ((0, 4), (12, 14), (14, 16))
 PIECES = 2
 AHEAD = 6
 FIRST_LAG = 2
 SECOND_LAG = 10
-SCATTER_FIRST, SCATTER_LAST = 2, 12
+SCATTER_FIRST, SCATTER_LAST = 4, 12
 MESH = pl.DeviceIdType.MESH
 F32 = jnp.float32
 BF16 = jnp.bfloat16
@@ -171,11 +171,35 @@
             parts.append([fa * a[o + h * UNIT:o + (h + 1) * UNIT, :] + fb * b[o + h * UNIT:o + (h + 1) * UNIT, :] for o in (0, ROWS)])
         return tile, parts, totals
 
+    sequence = lax.broadcasted_iota(jnp.int32, (UNIT, 128), 0)
+
+    def pack(tile, totals):
+        spots = jnp.zeros((UNIT, 128), F32)
+        for h in range(HEADS):
+            spots = jnp.where(lane == h * UNIT + sequence, tile[:, h:h + 1], spots)
+            spots = jnp.where(lane == ROWS + h * UNIT + sequence, totals[h], spots)
+        return jnp.sum(spots, axis=0, keepdims=True)
+
+    def unpack(row):
+        spots = jnp.broadcast_to(row, (UNIT, 128))
+        columns = [jnp.sum(jnp.where(lane == n * UNIT + sequence, spots, 0.0), axis=1, keepdims=True) for n in range(2 * HEADS)]
+        return columns[:HEADS], columns[HEADS:]
+
+    def merge_packed(a, b):
+        (tops_a, totals_a), (tops_b, totals_b) = unpack(a[2 * ROWS:2 * ROWS + 1, :]), unpack(b[2 * ROWS:2 * ROWS + 1, :])
+        parts, totals = [], []
+        for h in range(HEADS):
+            top = jnp.maximum(tops_a[h], tops_b[h])
+            fa, fb = jnp.exp(tops_a[h] - top), jnp.exp(tops_b[h] - top)
+            totals.append(fa * totals_a[h] + fb * totals_b[h])
+            parts.append([fa * a[o + h * UNIT:o + (h + 1) * UNIT, :] + fb * b[o + h * UNIT:o + (h + 1) * UNIT, :] for o in (0, ROWS)])
+        return parts, totals
+
     def first_copy(j):
         return pltpu.make_async_remote_copy(pk.at[j, 1 - core], rc1.at[j], s1.at[j], r1.at[j], device_id=beside, device_id_type=MESH)
 
     def second_copy(j):
-        rows = ch.at[j, x_side]
+        rows = ch.at[j, x_side, pl.ds(0, 2 * ROWS + 1)]
         return pltpu.make_async_remote_copy(rows, rows, s2.at[j], r2.at[j], device_id=over, device_id_type=MESH)
 
     def either(condition, yes, no):
@@ -196,8 +220,7 @@
             for h in range(HEADS):
                 ch[n, x_side, h * UNIT:(h + 1) * UNIT, :] = parts[h][0]
                 ch[n, x_side, ROWS + h * UNIT:ROWS + (h + 1) * UNIT, :] = parts[h][1]
-                tile = jnp.where(lane == HEADS + h, totals[h], tile)
-            ch[n, x_side, 2 * ROWS:, :] = tile
+            ch[n, x_side, 2 * ROWS:2 * ROWS + 1, :] = pack(tile, totals)
 
         def both():
             for n in pair:
@@ -218,8 +241,8 @@
     def finish(*chunk_ids):
         for n in chunk_ids:
             second_copy(n).wait_recv()
-        merged = [merge(ch[n, 0], ch[n, 1]) for n in chunk_ids]
-        for n, (_, parts, totals) in zip(chunk_ids, merged):
+        merged = [merge_packed(ch[n, 0], ch[n, 1]) for n in chunk_ids]
+        for n, (parts, totals) in zip(chunk_ids, merged):
             rows = pl.ds(final_block(n) * UNIT, UNIT)
             for h in range(HEADS):
                 inverse = 1.0 / totals[h]

time: 37.9 us -> 37.3 us (0.984)
  Pallas kernels: 37.1 us -> 36.5 us
    pallas_call x1, Pallas kernels: 25.3 us -> 24.7 us  [local_step(): pl.pallas_call(functools.partial(attend_kernel, window), out_shape=(*[plt...]
where the time goes in v11:
time: 37.3 us; the launch traced here: 37.1 us
  Pallas kernels  36.5 us (98%)
  between operations  0.66 us (2%)
    pallas_call x1, Pallas kernels, local_step(): pl.pallas_call(functools.partial(attend_kernel, window), out_shape=(*[plt...  24.7 us
    pallas_call x1, Pallas kernels, local_step(): pl.pallas_call(functools.partial(write_kernel, window), out_shape=(jax.Sh...  11.8 us

profile of v11, /device:TPU:0, one launch (start us, length us, event | category | flops | bytes accessed | tf_op | source)
XLA Modules:
  0.0 37.1 jit_solution(13439870408510477566)
XLA Ops:
  0.6 0.0 copy-start
  0.6 24.7 %attend.1 = (bf16[128,128,256]{2,1,0:T(8,128)(2,1)S(1)}, bf16[128,128,256]{2,1,0:T(8,128)(2,1)S(1)}, bf16[128,128,256]{2,1,0:T(8,128)(2,1)S(1)}, bf16[128,128,25...) custom-call(s32[2,128]{1,0:T(2,128)} %bitcast.1, ...), custom_call_target="tpu_custom_call" | custom-call | tf_op jit(solution)/shard_map/attend/pallas_call | solution.py:450
  25.3 0.0 copy-done
  25.3 11.8 %write.1 = (bf16[256,640]{1,0:T(8,128)(2,1)}, bf16[256,128,256]{2,1,0:T(8,128)(2,1)}, bf16[256,128,256]{2,1,0:T(8,128)(2,1)}, s32[256,128]{1,0:T(8,128)}) custom-call(s32[256]{0:T(256)S(1)} %copy-done, f32[256,256]{1,0:T(8,128)S(1)} %get-tuple-element.12.k_new, f32[256,256]{1,0:T(8,128)S(1)} %get-tuple-element.13.v_new, ...), custom_call_target="tpu_custom_call" | custom-call | tf_op jit(solution)/shard_map/write/pallas_call | solution.py:470
Async XLA Ops:
  0.6 24.7 %copy-start = (s32[256]{0:T(256)S(1)}, s32[256]{0:T(256)}, u32[]{:S(2)}) copy-start(s32[256]{0:T(256)} %pos.1) | copy-start | bytes 3076

commit v12 on v11

--- a/solution.py
+++ b/solution.py
@@ -24,7 +24,6 @@
 PIECES = 2
 AHEAD = 6
 FIRST_LAG = 2
-SECOND_LAG = 10
 SCATTER_FIRST, SCATTER_LAST = 4, 12
 MESH = pl.DeviceIdType.MESH
 F32 = jnp.float32
@@ -313,10 +312,6 @@
         def _():
             first_merge(j - FIRST_LAG)
 
-        @pl.when(j >= SECOND_LAG)
-        def _():
-            second_merge(j - SECOND_LAG)
-
         for ahead in range(PIECES):
             @pl.when((j + AHEAD < chunks) & ((j + AHEAD) // span == ahead))
             def _():
@@ -330,31 +325,9 @@
         lax.fori_loop(piece * span // 2, (piece + 1) * span // 2, functools.partial(step, piece), 0)
     for small in smalls[8:]:
         small.wait()
-    seconds = list(range(chunks - SECOND_LAG, chunks, 2))
-    firsts = list(range(chunks - FIRST_LAG, chunks, 2))
-
-    def second_upto(last):
-        while seconds and seconds[0] < last:
-            second_merge(seconds.pop(0))
-
-    second_upto(SCATTER_GROUPS[0][1])
-    project_scattered(0)
-    for j in firsts:
-        first_merge(j)
-    project_whole(0)
-    second_upto(SCATTER_GROUPS[1][1])
-    project_scattered(1)
-    forward(0)
-    collect_whole(0)
-    for g in range(1, len(WHOLE_GROUPS)):
-        second_upto(WHOLE_GROUPS[g][1])
-        project_whole(g)
-        if g == 1:
-            collect_scattered(0)
-    forward(1)
-    collect_scattered(1)
-    for g in range(1, len(WHOLE_GROUPS)):
-        collect_whole(g)
+    def second_merges(first, last):
+        for j in range(first, last, 2):
+            second_merge(j)
 
     def drain(j, carry):
         first_copy(j).wait_send()
@@ -364,7 +337,26 @@
             second_copy(j).wait_send()
         return carry
 
+    second_merges(*SCATTER_GROUPS[0])
+    project_scattered(0)
+    for j in range(chunks - FIRST_LAG, chunks, 2):
+        first_merge(j)
+    second_merges(*WHOLE_GROUPS[0])
+    project_whole(0)
+    second_merges(*SCATTER_GROUPS[1])
+    project_scattered(1)
+    forward(0)
+    collect_whole(0)
+    second_merges(*WHOLE_GROUPS[1])
+    project_whole(1)
+    collect_scattered(0)
     lax.fori_loop(0, chunks, drain, 0)
+    second_merges(*WHOLE_GROUPS[2])
+    project_whole(2)
+    forward(1)
+    collect_whole(1)
+    collect_scattered(1)
+    collect_whole(2)
     for group in gathers:
         for gather in group:
             gather.wait_send()
@@ -399,21 +391,20 @@
             for copy in copies(j - depth):
                 copy.wait()
 
-        def group(i, carry):
-            for n in range(8):
-                row = i * 8 + n
-                b = j * chunk + row
-                slot = (pos[b] & (window - 1)) - me * slots
-                base = pl.multiple_of((jnp.clip(slot, 0, slots - 1) // 16) * 16, 16)
-                for new, cache, out in ((k_new, k_vm[piece], k_ring), (v_new, v_vm[piece], v_ring)):
+        for n, (new, cache, out) in enumerate(((k_new, k_vm[piece], k_ring), (v_new, v_vm[piece], v_ring))):
+            def group(i, carry):
+                for m in range(8):
+                    row = i * 8 + m
+                    b = j * chunk + row
+                    slot = (pos[b] & (window - 1)) - me * slots
+                    base = pl.multiple_of((jnp.clip(slot, 0, slots - 1) // 16) * 16, 16)
                     out[ring, row] = cache[b - piece * part]
                     fresh = jnp.broadcast_to(new[pl.ds(b, 1), :], (16, HEAD_DIM))
                     old = cache[b - piece * part, pl.ds(base, 16), :].astype(F32)
                     out[ring, row, pl.ds(base, 16), :] = jnp.where(tile_row == slot - base, fresh, old).astype(BF16)
-            return carry
-        lax.fori_loop(0, chunk // 8, group, 0)
-        for copy in copies(j):
-            copy.start()
+                return carry
+            lax.fori_loop(0, chunk // 8, group, 0)
+            copies(j)[n].start()
         return carry
 
     for piece in range(PIECES):

time: 37.3 us -> 36.9 us (0.989)
  Pallas kernels: 36.5 us -> 36.1 us
where the time goes in v12:
time: 36.9 us; the launch traced here: 36.8 us
  Pallas kernels  36.1 us (98%)
  between operations  0.66 us (2%)
    pallas_call x1, Pallas kernels, local_step(): pl.pallas_call(functools.partial(attend_kernel, window), out_shape=(*[plt...  24.4 us
    pallas_call x1, Pallas kernels, local_step(): pl.pallas_call(functools.partial(write_kernel, window), out_shape=(jax.Sh...  11.7 us

profile of v12, /device:TPU:0, one launch (start us, length us, event | category | flops | bytes accessed | tf_op | source)
XLA Modules:
  0.0 36.8 jit_solution(2986525672356990093)
XLA Ops:
  0.6 0.0 copy-start
  0.6 24.4 %attend.1 = (bf16[128,128,256]{2,1,0:T(8,128)(2,1)S(1)}, bf16[128,128,256]{2,1,0:T(8,128)(2,1)S(1)}, bf16[128,128,256]{2,1,0:T(8,128)(2,1)S(1)}, bf16[128,128,25...) custom-call(s32[2,128]{1,0:T(2,128)} %bitcast.1, ...), custom_call_target="tpu_custom_call" | custom-call | tf_op jit(solution)/shard_map/attend/pallas_call | solution.py:441
  25.1 0.0 copy-done
  25.1 11.7 %write.1 = (bf16[256,640]{1,0:T(8,128)(2,1)}, bf16[256,128,256]{2,1,0:T(8,128)(2,1)}, bf16[256,128,256]{2,1,0:T(8,128)(2,1)}, s32[256,128]{1,0:T(8,128)}) custom-call(s32[256]{0:T(256)S(1)} %copy-done, f32[256,256]{1,0:T(8,128)S(1)} %get-tuple-element.12.k_new, f32[256,256]{1,0:T(8,128)S(1)} %get-tuple-element.13.v_new, ...), custom_call_target="tpu_custom_call" | custom-call | tf_op jit(solution)/shard_map/write/pallas_call | solution.py:461
Async XLA Ops:
  0.6 24.4 %copy-start = (s32[256]{0:T(256)S(1)}, s32[256]{0:T(256)}, u32[]{:S(2)}) copy-start(s32[256]{0:T(256)} %pos.1) | copy-start | bytes 3076

commit v13 on v12

--- a/solution.py
+++ b/solution.py
@@ -75,11 +75,16 @@
         row = pos[r:r + 1, :].astype(F32)
         pos_b[pl.ds(128 * r, 128), :] = jnp.transpose(jnp.broadcast_to(row, (128, 128)))
     read_ahead(1, 2)
-    angles = pos_b[...] * freq[...]
-    low = lax.broadcasted_iota(jnp.int32, (batch, 128), 1) < ROPE_DIM // 2
-    cos_t = jnp.cos(angles)
-    sin_t = jnp.sin(angles)
-    sin_t = jnp.where(low, -sin_t, sin_t)
+    half = batch // 2
+    low = lax.broadcasted_iota(jnp.int32, (half, 128), 1) < ROPE_DIM // 2
+    angles = jnp.where(low, pos_b[:half, :], pos_b[half:, :]) * freq[...]
+
+    def spread_halves(table, sign):
+        turned = pltpu.roll(table, ROPE_DIM // 2, 1)
+        return jnp.concatenate([jnp.where(low, sign * table, turned), jnp.where(low, sign * turned, table)], axis=0)
+
+    cos_t = spread_halves(jnp.cos(angles), 1.0)
+    sin_t = spread_halves(jnp.sin(angles), -1.0)
 
     def rotate(first):
         return first * cos_t + pltpu.roll(first, ROPE_DIM // 2, 1) * sin_t

time: 36.9 us -> 36.9 us (level)
  no operation moved by 1% of the time
where the time goes in v13:
time: 36.9 us; the launch traced here: 36.8 us
  Pallas kernels  36.1 us (98%)
  between operations  0.66 us (2%)
    pallas_call x1, Pallas kernels, local_step(): pl.pallas_call(functools.partial(attend_kernel, window), out_shape=(*[plt...  24.4 us
    pallas_call x1, Pallas kernels, local_step(): pl.pallas_call(functools.partial(write_kernel, window), out_shape=(jax.Sh...  11.7 us

profile of v13, /device:TPU:0, one launch (start us, length us, event | category | flops | bytes accessed | tf_op | source)
XLA Modules:
  0.0 36.8 jit_solution(11040899548011532439)
XLA Ops:
  0.6 0.0 copy-start
  0.6 24.4 %attend.1 = (bf16[128,128,256]{2,1,0:T(8,128)(2,1)S(1)}, bf16[128,128,256]{2,1,0:T(8,128)(2,1)S(1)}, bf16[128,128,256]{2,1,0:T(8,128)(2,1)S(1)}, bf16[128,128,25...) custom-call(s32[2,128]{1,0:T(2,128)} %bitcast.1, ...), custom_call_target="tpu_custom_call" | custom-call | tf_op jit(solution)/shard_map/attend/pallas_call | solution.py:446
  25.1 0.0 copy-done
  25.1 11.7 %write.1 = (bf16[256,640]{1,0:T(8,128)(2,1)}, bf16[256,128,256]{2,1,0:T(8,128)(2,1)}, bf16[256,128,256]{2,1,0:T(8,128)(2,1)}, s32[256,128]{1,0:T(8,128)}) custom-call(s32[256]{0:T(256)S(1)} %copy-done, f32[256,256]{1,0:T(8,128)S(1)} %get-tuple-element.12.k_new, f32[256,256]{1,0:T(8,128)S(1)} %get-tuple-element.13.v_new, ...), custom_call_target="tpu_custom_call" | custom-call | tf_op jit(solution)/shard_map/write/pallas_call | solution.py:466
Async XLA Ops:
  0.6 24.4 %copy-start = (s32[256]{0:T(256)S(1)}, s32[256]{0:T(256)}, u32[]{:S(2)}) copy-start(s32[256]{0:T(256)} %pos.1) | copy-start | bytes 3076

commit v14 on v13

--- a/solution.py
+++ b/solution.py
@@ -67,14 +67,13 @@
 
     for small in smalls[:8]:
         small.start()
-    read_ahead(0, 1)
+    read_ahead(0, 2)
 
     smalls[0].wait()
     smalls[1].wait()
     for r in range(batch // 128):
         row = pos[r:r + 1, :].astype(F32)
         pos_b[pl.ds(128 * r, 128), :] = jnp.transpose(jnp.broadcast_to(row, (128, 128)))
-    read_ahead(1, 2)
     half = batch // 2
     low = lax.broadcasted_iota(jnp.int32, (half, 128), 1) < ROPE_DIM // 2
     angles = jnp.where(low, pos_b[:half, :], pos_b[half:, :]) * freq[...]
@@ -91,7 +90,7 @@
 
     smalls[2].wait()
     smalls[3].wait()
-    read_ahead(2, AHEAD)
+    read_ahead(2, 4)
     x32 = x_in[...].astype(F32)
     x_f[...] = x32
     mean_sq = jnp.mean(x32 * x32, axis=-1, keepdims=True)
@@ -103,6 +102,7 @@
     k_new[:, 128:] = k_row[:, 128:].astype(BF16).astype(F32)
     v_new[...] = jnp.dot(normed, wv[...], preferred_element_type=F32).astype(BF16).astype(F32)
     smalls[6].wait()
+    read_ahead(4, AHEAD)
     for small in smalls[8:]:
         small.start()
     for h in range(HEADS):

time: 36.9 us -> 37 us (level)
  no operation moved by 1% of the time
where the time goes in v14:
time: 37 us; the launch traced here: 36.8 us
  Pallas kernels  36.2 us (98%)
  between operations  0.66 us (2%)
    pallas_call x1, Pallas kernels, local_step(): pl.pallas_call(functools.partial(attend_kernel, window), out_shape=(*[plt...  24.5 us
    pallas_call x1, Pallas kernels, local_step(): pl.pallas_call(functools.partial(write_kernel, window), out_shape=(jax.Sh...  11.7 us

profile of v14, /device:TPU:0, one launch (start us, length us, event | category | flops | bytes accessed | tf_op | source)
XLA Modules:
  0.0 36.8 jit_solution(7328183758621000409)
XLA Ops:
  0.6 0.0 copy-start
  0.6 24.5 %attend.1 = (bf16[128,128,256]{2,1,0:T(8,128)(2,1)S(1)}, bf16[128,128,256]{2,1,0:T(8,128)(2,1)S(1)}, bf16[128,128,256]{2,1,0:T(8,128)(2,1)S(1)}, bf16[128,128,25...) custom-call(s32[2,128]{1,0:T(2,128)} %bitcast.1, ...), custom_call_target="tpu_custom_call" | custom-call | tf_op jit(solution)/shard_map/attend/pallas_call | solution.py:446
  25.1 0.0 copy-done
  25.1 11.7 %write.1 = (bf16[256,640]{1,0:T(8,128)(2,1)}, bf16[256,128,256]{2,1,0:T(8,128)(2,1)}, bf16[256,128,256]{2,1,0:T(8,128)(2,1)}, s32[256,128]{1,0:T(8,128)}) custom-call(s32[256]{0:T(256)S(1)} %copy-done, f32[256,256]{1,0:T(8,128)S(1)} %get-tuple-element.12.k_new, f32[256,256]{1,0:T(8,128)S(1)} %get-tuple-element.13.v_new, ...), custom_call_target="tpu_custom_call" | custom-call | tf_op jit(solution)/shard_map/write/pallas_call | solution.py:466
Async XLA Ops:
  0.6 24.5 %copy-start = (s32[256]{0:T(256)S(1)}, s32[256]{0:T(256)}, u32[]{:S(2)}) copy-start(s32[256]{0:T(256)} %pos.1) | copy-start | bytes 3076
